TPU v7x, 8 devices: a whole 2x2x1 slice. The times are simulated.
8 devices in a mesh: col: 4 (over z, y, x), row: 2 (over core).
Axes of the slice: x: 2, y: 2, z: 1, core: 2. Of those that a mesh axis runs over, the one named last changes fastest.
Arguments:
- matrix: bfloat16 [11264, 11264], P('row', 'col')
- y_start: float32 [11264, 64], P(('col', 'row'))
- center: float32 [], replicated
- half_width: float32 [], replicated
Outputs:
- output 1: float32 [11264, 64], P(('col', 'row'))
- output 2: float32 [64, 64], replicated
All inputs are finite; a program needn't handle non-finite values.
Results may differ from a plain program's by a relative error of at most 0.0144715.
Values are sent between devices in bfloat16 or wider.
A program may use at most 1 GiB of HBM per device.

v0:
```python
import jax
import jax.numpy as jnp
from jax import lax
from jax.sharding import PartitionSpec as P

DEGREE = 8


def solution(mesh):
    row_count = mesh.shape["row"]
    col_count = mesh.shape["col"]
    both_axes = ("col", "row")
    realign_pairs = [(col_idx * row_count + row_idx, row_idx * col_count + col_idx) for row_idx in range(row_count) for col_idx in range(col_count)]

    def apply_matrix(mat_tile, y_low):
        src_block = lax.all_gather(y_low, "row", axis=0, tiled=True)
        part_sum = jnp.dot(mat_tile, src_block, preferred_element_type=jnp.float32)
        folded = lax.psum_scatter(part_sum, "col", scatter_dimension=0, tiled=True)
        return lax.ppermute(folded, both_axes, realign_pairs)

    def local_filter(mat_tile, y_start, center, half_width):
        y_prev = y_start
        y_cur = (apply_matrix(mat_tile, y_start.astype(jnp.bfloat16)) - center * y_start) / half_width
        for step_index in range(DEGREE - 1):
            y_next = 2.0 * (apply_matrix(mat_tile, y_cur.astype(jnp.bfloat16)) - center * y_cur) / half_width - y_prev
            y_prev = y_cur
            y_cur = y_next
        y_low = y_cur.astype(jnp.bfloat16)
        image_low = apply_matrix(mat_tile, y_low).astype(jnp.bfloat16)
        local_gram = jnp.einsum("pa,pb->ab", y_low, image_low, preferred_element_type=jnp.float32)
        gram_mat = lax.psum(local_gram, both_axes) / (mat_tile.shape[0] * row_count)
        return y_cur, gram_mat

    return jax.shard_map(local_filter, mesh=mesh, in_specs=(P("row", "col"), P(both_axes, None), P(), P()), out_specs=(P(both_axes, None), P()), check_vma=False)
```

profile of v0, /device:TPU:0, one launch (start us, length us, event | category | flops | bytes accessed | tf_op | source)
XLA Modules:
  0.0 544.4 jit_solution(9660516655522107286)
XLA Ops:
  7.2 1.0 convert_element_type.30
  8.3 2.6 all_gather.27
  10.8 16.5 %fusion.10 = f32[5632,64]{0,1:T(8,128)} fusion(bf16[5632,2816]{1,0:T(8,128)(2,1)} %param.4, bf16[2816,64]{0,1:T(8,128)(2,1)S(1)} %all_gather.27), kind=kOutput, calls=%fused_computation.27 | convolution fusion | flops 2030043136 | bytes 33521664 | tf_op jit(solution)/shard_map/dot_general | solution.py:17
  27.4 27.2 %reduce-scatter.10.cloned.1.call-done = f32[1408,64]{0,1:T(8,128)} async-done(((f32[5632,64]{0,1:T(8,128)}), f32[1408,64]{0,1:T(8,128)}) %reduce-scatter.10.cloned.1.call-update) | async-done | bytes 360464 | tf_op jit(solution)/shard_map/reduce_scatter | solution.py:18
  54.6 1.6 collective-permute-start
  57.5 0.1 fusion.3
  57.6 11.1 %all_gather.28 = bf16[2816,64]{0,1:T(8,128)(2,1)S(1)} all-gather(bf16[1408,64]{0,1:T(8,128)(2,1)S(1)} %fusion.3), channel_id=1, replica_groups=mesh['col'=4,'row'=2] {'row'}, dimensions={0}, use_global_device_ids=true | all-gather | bytes 540672 | tf_op jit(solution)/shard_map/all_gather | solution.py:16
  68.7 16.2 %convolution_bitcast_fusion.7 = f32[5632,64]{0,1:T(8,128)} fusion(bf16[2816,64]{0,1:T(8,128)(2,1)S(1)} %all_gather.28, bf16[5632,2816]{1,0:T(8,128)(2,1)} %param.4), kind=kOutput, calls=%fused_computation.7 | convolution fusion | flops 2030043136 | bytes 33521664 | tf_op jit(solution)/shard_map/dot_general | solution.py:17
  85.0 25.4 %reduce-scatter.12.cloned.1.call-done = f32[1408,64]{0,1:T(8,128)} async-done(((f32[5632,64]{0,1:T(8,128)}), f32[1408,64]{0,1:T(8,128)}) %reduce-scatter.12.cloned.1.call-update) | async-done | bytes 360464 | tf_op jit(solution)/shard_map/reduce_scatter | solution.py:18
  110.4 1.6 collective-permute-start.1
  112.1 0.1 fusion.9
  112.2 12.4 %all_gather.29 = bf16[2816,64]{0,1:T(8,128)(2,1)S(1)} all-gather(bf16[1408,64]{0,1:T(8,128)(2,1)S(1)} %get-tuple-element.12), channel_id=1, replica_groups=mesh['col'=4,'row'=2] {'row'}, dimensions={0}, use_global_device_ids=true | all-gather | bytes 540672 | tf_op jit(solution)/shard_map/all_gather | solution.py:16
  124.6 16.2 %convolution_bitcast_fusion.6 = f32[5632,64]{0,1:T(8,128)} fusion(bf16[2816,64]{0,1:T(8,128)(2,1)S(1)} %all_gather.29, bf16[5632,2816]{1,0:T(8,128)(2,1)} %param.4), kind=kOutput, calls=%fused_computation.6 | convolution fusion | flops 2030043136 | bytes 33521664 | tf_op jit(solution)/shard_map/dot_general | solution.py:17
  140.9 25.4 %reduce-scatter.14.cloned.1.call-done = f32[1408,64]{0,1:T(8,128)} async-done(((f32[5632,64]{0,1:T(8,128)}), f32[1408,64]{0,1:T(8,128)}) %reduce-scatter.14.cloned.1.call-update) | async-done | bytes 360464 | tf_op jit(solution)/shard_map/reduce_scatter | solution.py:18
  166.3 1.6 collective-permute-start.2
  167.9 0.1 fusion.8
  168.1 12.4 %all_gather.30 = bf16[2816,64]{0,1:T(8,128)(2,1)S(1)} all-gather(bf16[1408,64]{0,1:T(8,128)(2,1)S(1)} %get-tuple-element.10), channel_id=1, replica_groups=mesh['col'=4,'row'=2] {'row'}, dimensions={0}, use_global_device_ids=true | all-gather | bytes 540672 | tf_op jit(solution)/shard_map/all_gather | solution.py:16
  180.5 16.2 %convolution_bitcast_fusion.5 = f32[5632,64]{0,1:T(8,128)} fusion(bf16[2816,64]{0,1:T(8,128)(2,1)S(1)} %all_gather.30, bf16[5632,2816]{1,0:T(8,128)(2,1)} %param.4), kind=kOutput, calls=%fused_computation.5 | convolution fusion | flops 2030043136 | bytes 33521664 | tf_op jit(solution)/shard_map/dot_general | solution.py:17
  196.8 25.4 %reduce-scatter.16.cloned.1.call-done = f32[1408,64]{0,1:T(8,128)} async-done(((f32[5632,64]{0,1:T(8,128)}), f32[1408,64]{0,1:T(8,128)}) %reduce-scatter.16.cloned.1.call-update) | async-done | bytes 360464 | tf_op jit(solution)/shard_map/reduce_scatter | solution.py:18
  222.2 1.6 collective-permute-start.3
  223.8 0.1 fusion.7
  223.9 12.6 %all_gather.31 = bf16[2816,64]{0,1:T(8,128)(2,1)S(1)} all-gather(bf16[1408,64]{0,1:T(8,128)(2,1)S(1)} %get-tuple-element.8), channel_id=1, replica_groups=mesh['col'=4,'row'=2] {'row'}, dimensions={0}, use_global_device_ids=true | all-gather | bytes 540672 | tf_op jit(solution)/shard_map/all_gather | solution.py:16
  236.5 16.2 %convolution_bitcast_fusion.4 = f32[5632,64]{0,1:T(8,128)} fusion(bf16[2816,64]{0,1:T(8,128)(2,1)S(1)} %all_gather.31, bf16[5632,2816]{1,0:T(8,128)(2,1)} %param.4), kind=kOutput, calls=%fused_computation.4 | convolution fusion | flops 2030043136 | bytes 33521664 | tf_op jit(solution)/shard_map/dot_general | solution.py:17
  252.8 25.4 %reduce-scatter.18.cloned.1.call-done = f32[1408,64]{0,1:T(8,128)} async-done(((f32[5632,64]{0,1:T(8,128)}), f32[1408,64]{0,1:T(8,128)}) %reduce-scatter.18.cloned.1.call-update) | async-done | bytes 360464 | tf_op jit(solution)/shard_map/reduce_scatter | solution.py:18
  278.3 1.6 collective-permute-start.4
  279.9 0.1 fusion.6
  280.0 12.4 %all_gather.32 = bf16[2816,64]{0,1:T(8,128)(2,1)S(1)} all-gather(bf16[1408,64]{0,1:T(8,128)(2,1)S(1)} %get-tuple-element.6), channel_id=1, replica_groups=mesh['col'=4,'row'=2] {'row'}, dimensions={0}, use_global_device_ids=true | all-gather | bytes 540672 | tf_op jit(solution)/shard_map/all_gather | solution.py:16
  292.4 16.2 %convolution_bitcast_fusion.3 = f32[5632,64]{0,1:T(8,128)} fusion(bf16[2816,64]{0,1:T(8,128)(2,1)S(1)} %all_gather.32, bf16[5632,2816]{1,0:T(8,128)(2,1)} %param.4), kind=kOutput, calls=%fused_computation.3 | convolution fusion | flops 2030043136 | bytes 33521664 | tf_op jit(solution)/shard_map/dot_general | solution.py:17
  308.7 25.4 %reduce-scatter.20.cloned.1.call-done = f32[1408,64]{0,1:T(8,128)} async-done(((f32[5632,64]{0,1:T(8,128)}), f32[1408,64]{0,1:T(8,128)}) %reduce-scatter.20.cloned.1.call-update) | async-done | bytes 360464 | tf_op jit(solution)/shard_map/reduce_scatter | solution.py:18
  334.1 1.6 collective-permute-start.5
  335.7 0.1 fusion.5
  335.8 12.4 %all_gather.33 = bf16[2816,64]{0,1:T(8,128)(2,1)S(1)} all-gather(bf16[1408,64]{0,1:T(8,128)(2,1)S(1)} %get-tuple-element.4), channel_id=1, replica_groups=mesh['col'=4,'row'=2] {'row'}, dimensions={0}, use_global_device_ids=true | all-gather | bytes 540672 | tf_op jit(solution)/shard_map/all_gather | solution.py:16
  348.2 16.2 %convolution_bitcast_fusion.2 = f32[5632,64]{0,1:T(8,128)} fusion(bf16[2816,64]{0,1:T(8,128)(2,1)S(1)} %all_gather.33, bf16[5632,2816]{1,0:T(8,128)(2,1)} %param.4), kind=kOutput, calls=%fused_computation.2 | convolution fusion | flops 2030043136 | bytes 33521664 | tf_op jit(solution)/shard_map/dot_general | solution.py:17
  364.5 25.4 %reduce-scatter.22.cloned.1.call-done = f32[1408,64]{0,1:T(8,128)} async-done(((f32[5632,64]{0,1:T(8,128)}), f32[1408,64]{0,1:T(8,128)}) %reduce-scatter.22.cloned.1.call-update) | async-done | bytes 360464 | tf_op jit(solution)/shard_map/reduce_scatter | solution.py:18
  389.9 1.6 collective-permute-start.6
  391.6 0.1 fusion.2
  391.6 12.4 %all_gather.34 = bf16[2816,64]{0,1:T(8,128)(2,1)S(1)} all-gather(bf16[1408,64]{0,1:T(8,128)(2,1)S(1)} %fusion.2), channel_id=1, replica_groups=mesh['col'=4,'row'=2] {'row'}, dimensions={0}, use_global_device_ids=true | all-gather | bytes 540672 | tf_op jit(solution)/shard_map/all_gather | solution.py:16
  404.0 16.2 %convolution_bitcast_fusion.1 = f32[5632,64]{0,1:T(8,128)} fusion(bf16[2816,64]{0,1:T(8,128)(2,1)S(1)} %all_gather.34, bf16[5632,2816]{1,0:T(8,128)(2,1)} %param.4), kind=kOutput, calls=%fused_computation.1 | convolution fusion | flops 2030043136 | bytes 33521664 | tf_op jit(solution)/shard_map/dot_general | solution.py:17
  420.4 25.4 %reduce-scatter.24.cloned.1.call-done = f32[1408,64]{0,1:T(8,128)} async-done(((f32[5632,64]{0,1:T(8,128)}), f32[1408,64]{0,1:T(8,128)}) %reduce-scatter.24.cloned.1.call-update) | async-done | bytes 360464 | tf_op jit(solution)/shard_map/reduce_scatter | solution.py:18
  445.8 1.6 collective-permute-start.7
  447.4 0.9 fusion.4
  448.3 12.7 %all_gather.35 = bf16[2816,64]{0,1:T(8,128)(2,1)S(1)} all-gather(bf16[1408,64]{0,1:T(8,128)(2,1)S(1)} %get-tuple-element.2), channel_id=1, replica_groups=mesh['col'=4,'row'=2] {'row'}, dimensions={0}, use_global_device_ids=true | all-gather | bytes 540672 | tf_op jit(solution)/shard_map/all_gather | solution.py:16
  460.9 16.2 %convolution_bitcast_fusion = f32[5632,64]{0,1:T(8,128)} fusion(bf16[2816,64]{0,1:T(8,128)(2,1)S(1)} %all_gather.35, bf16[5632,2816]{1,0:T(8,128)(2,1)} %param.4), kind=kOutput, calls=%fused_computation | convolution fusion | flops 2030043136 | bytes 33521664 | tf_op jit(solution)/shard_map/dot_general | solution.py:17
  477.2 25.4 %reduce-scatter.26.cloned.1.call-done = f32[1408,64]{0,1:T(8,128)} async-done(((f32[5632,64]{0,1:T(8,128)}), f32[1408,64]{0,1:T(8,128)}) %reduce-scatter.26.cloned.1.call-update) | async-done | bytes 360464 | tf_op jit(solution)/shard_map/reduce_scatter | solution.py:18
  502.6 1.6 collective-permute-start.8
  504.2 0.2 fusion
  504.4 32.8 %psum.7 = f32[64,64]{1,0:T(8,128)S(1)} all-reduce(f32[64,64]{1,0:T(8,128)S(1)} %fusion), channel_id=1, replica_groups=mesh['col'=4,'row'=2] {'col','row'}, use_global_device_ids=true, to_apply=%region_9.0 | all-reduce | flops 4096 | bytes 32768 | tf_op jit(solution)/shard_map/psum | solution.py:31
  537.3 0.6 broadcast_multiply_fusion
  (29 shorter events, 0.5 us)
Async XLA Ops:
  7.2 50.4 %copy-start = (f32[1408,64]{0,1:T(8,128)S(1)}, f32[1408,64]{0,1:T(8,128)}, u32[]{:S(2)}) copy-start(f32[1408,64]{0,1:T(8,128)} %param.5) | copy-start | bytes 1081348
  7.2 47.4 %reduce-scatter.10.cloned.1.call-start = ((), (), s32[]{:S(2)}) async-start(), calls=%async_computation.9 | async-start | bytes 1802240 | tf_op jit(solution)/shard_map/reduce_scatter | solution.py:18
  27.4 83.0 %reduce-scatter.12.cloned.1.call-start = ((), (), s32[]{:S(2)}) async-start(), calls=%async_computation.10 | async-start | bytes 1802240 | tf_op jit(solution)/shard_map/reduce_scatter | solution.py:18
  54.6 2.9 collective-permute-start
  85.0 81.3 %reduce-scatter.14.cloned.1.call-start = ((), (), s32[]{:S(2)}) async-start(), calls=%async_computation.11 | async-start | bytes 1802240 | tf_op jit(solution)/shard_map/reduce_scatter | solution.py:18
  110.4 1.6 collective-permute-start.1
  140.9 81.3 %reduce-scatter.16.cloned.1.call-start = ((), (), s32[]{:S(2)}) async-start(), calls=%async_computation.12 | async-start | bytes 1802240 | tf_op jit(solution)/shard_map/reduce_scatter | solution.py:18
  166.3 1.6 collective-permute-start.2
  196.8 81.5 %reduce-scatter.18.cloned.1.call-start = ((), (), s32[]{:S(2)}) async-start(), calls=%async_computation.13 | async-start | bytes 1802240 | tf_op jit(solution)/shard_map/reduce_scatter | solution.py:18
  222.2 1.6 collective-permute-start.3
  252.8 81.3 %reduce-scatter.20.cloned.1.call-start = ((), (), s32[]{:S(2)}) async-start(), calls=%async_computation.14 | async-start | bytes 1802240 | tf_op jit(solution)/shard_map/reduce_scatter | solution.py:18
  278.3 1.6 collective-permute-start.4
  308.7 81.3 %reduce-scatter.22.cloned.1.call-start = ((), (), s32[]{:S(2)}) async-start(), calls=%async_computation.15 | async-start | bytes 1802240 | tf_op jit(solution)/shard_map/reduce_scatter | solution.py:18
  334.1 1.6 collective-permute-start.5
  364.5 81.3 %reduce-scatter.24.cloned.1.call-start = ((), (), s32[]{:S(2)}) async-start(), calls=%async_computation.16 | async-start | bytes 1802240 | tf_op jit(solution)/shard_map/reduce_scatter | solution.py:18
  389.9 1.6 collective-permute-start.6
  420.3 82.3 %reduce-scatter.26.cloned.1.call-start = ((), (), s32[]{:S(2)}) async-start(), calls=%async_computation.17 | async-start | bytes 1802240 | tf_op jit(solution)/shard_map/reduce_scatter | solution.py:18
  445.8 1.6 collective-permute-start.7
  502.6 1.6 collective-permute-start.8
Sparse Core Ops, SparseCore 0:
  27.5 27.0 reduce-scatter.9
  85.1 25.2 reduce-scatter.11
  141.0 25.2 reduce-scatter.13
  196.9 25.2 reduce-scatter.15
  252.9 25.3 reduce-scatter.17
  308.8 25.2 reduce-scatter.19
  364.6 25.2 reduce-scatter.21
  420.4 25.2 reduce-scatter.23
  477.3 25.2 reduce-scatter.25
where the time goes:
time: 545 us; the launch traced here: 544 us
  waiting for transfers between devices  231 us (42%)
  matrix products  147 us (27%)
  blocking collectives  134 us (25%)
  between operations  15.2 us (3%)
  starting transfers between devices  15 us (3%)
    reduce_scatter x9, waiting for transfers between devices, apply_matrix(): folded = lax.psum_scatter(part_sum, 'col', scatter_dimension=0, tiled=True)  230 us
    dot_general x9, matrix products, apply_matrix(): part_sum = jnp.dot(mat_tile, src_block, preferred_element_type=jnp.float32)  146 us
    all_gather x9, blocking collectives, apply_matrix(): src_block = lax.all_gather(y_low, 'row', axis=0, tiled=True)  101 us
    psum x1, blocking collectives, local_filter(): gram_mat = lax.psum(local_gram, both_axes) / (mat_tile.shape[0] * row_count)  32.8 us
    ppermute x9, starting transfers between devices, apply_matrix(): return lax.ppermute(folded, both_axes, realign_pairs)  14.7 us
  transfers between devices with their start and end apart: 18, of which 9 were waited for; matrix products, arithmetic and copies ran while one was open for 0% of the time, Pallas kernels for 0%

commit v1 on v0

v1 whole, which is shorter than its diff:
```python
import functools

import jax
import jax.numpy as jnp
from jax import lax
from jax.experimental import pallas as pl
from jax.experimental.pallas import tpu as pltpu
from jax.sharding import PartitionSpec as P

DEGREE = 8
WIDTHS = (512, 512, 384)
OFFSETS = (0, 512, 1024)
CHUNKS = len(WIDTHS)
MESH = pl.DeviceIdType.MESH


def filter_kernel(piece, width, a_ref, y0_ref, c_ref, e_ref, y_out, g_out, tile, src, state, acc, psend, prec, gall, tile_sem, recv_sem, send_sem, fwd_sem, psend_sem, prec_sem, gsend_sem, grecv_sem, y_sem):
    chip = lax.axis_index("col")
    core = lax.axis_index("row")
    me = chip * 2 + core
    sibling = 1 - core
    chip_bit = lax.rem(chip, 2)
    chip_x = chip + 1 - 2 * chip_bit
    chip_y = lax.rem(chip + 2, 4)
    group = chip // 2
    near = core == group
    far = core != group
    near_int = 1 - lax.abs(core - group)

    own_dest = 2 * chip_bit + core
    own_slot = near_int * own_dest + (1 - near_int) * 4
    pair_first = 2 * chip_bit
    pair_second = 2 * (1 - chip_bit)
    fwd_slot = near_int * pair_second + (1 - near_int) * (pair_first + 1)
    fwd_chip = near_int * chip_y + (1 - near_int) * chip_x
    sib_slot = pair_first + sibling

    def local_load(order, slot, half):
        col = half * core + (1 - half) * sibling
        c = order
        rows = pl.ds(pl.multiple_of(slot * piece + OFFSETS[c], 128), WIDTHS[c])
        return pltpu.make_async_copy(
            a_ref.at[rows, pl.ds(pl.multiple_of(col * piece, 128), piece)],
            tile.at[rows, pl.ds(half * piece, piece)],
            tile_sem.at[slot, c, half],
        )

    def slot_view(par, slot, c):
        return src.at[par, slot, :, pl.ds(OFFSETS[c], WIDTHS[c])]

    def remote(src_view, dst_view, ssem, rsem, dev):
        return pltpu.make_async_remote_copy(src_ref=src_view, dst_ref=dst_view, send_sem=ssem, recv_sem=rsem, device_id=dev, device_id_type=MESH)

    def own_copy(par, c, d):
        dev = ((chip_x, group), (chip_y, group), (chip, group))[d]
        return remote(slot_view(par, own_slot, c), slot_view(par, own_dest, c), send_sem.at[d, c], recv_sem.at[par, own_dest, c], dev)

    def fwd_copy(par, c):
        return remote(slot_view(par, fwd_slot, c), slot_view(par, fwd_slot, c), fwd_sem.at[c], recv_sem.at[par, fwd_slot, c], (fwd_chip, core))

    def wait_slot(par, slot, c):
        view = slot_view(par, slot, c)
        remote(view, view, fwd_sem.at[c], recv_sem.at[par, slot, c], (chip, core)).wait_recv()

    def partial_copy(par, o):
        cols = pl.ds(OFFSETS[o], WIDTHS[o])
        return remote(psend.at[:, cols], prec.at[par, :, cols], psend_sem.at[o], prec_sem.at[par, o], (chip, sibling))

    def send_own(par, c):
        own_copy(par, c, 0).start()
        own_copy(par, c, 1).start()

        @pl.when(far)
        def _():
            own_copy(par, c, 2).start()

    def wait_own_sends(par, c):
        own_copy(par, c, 0).wait_send()
        own_copy(par, c, 1).wait_send()

        @pl.when(far)
        def _():
            own_copy(par, c, 2).wait_send()

    for pair in (pair_first, pair_second):
        for c in range(CHUNKS):
            for k in range(2):
                for half in range(2):
                    local_load(c, pair + k, half).start()

    barrier = pltpu.get_barrier_semaphore()
    for d in range(1, 8):
        other = lax.rem(me + d, 8)
        pl.semaphore_signal(barrier, inc=1, device_id=(other // 2, lax.rem(other, 2)), device_id_type=MESH)

    y0_copy = pltpu.make_async_copy(y0_ref, state.at[0], y_sem)
    y0_copy.start()
    state[1] = jnp.zeros_like(state[1])
    y0_copy.wait()
    src[0, own_slot] = state[0].astype(jnp.bfloat16)
    pl.semaphore_wait(barrier, 7)
    for c in range(CHUNKS):
        send_own(0, c)

    def product(par, pair, c, cols):
        total = None
        for k in range(2):
            rows = pl.ds(pl.multiple_of((pair + k) * piece + OFFSETS[c], 128), WIDTHS[c])
            left = src[par, pair + k, :, pl.ds(OFFSETS[c], WIDTHS[c])]
            part = jnp.dot(left, tile[rows, cols], preferred_element_type=jnp.float32)
            total = part if total is None else total + part
        return total

    def apply_matrix(t, par, first, combine):
        for step, pair in enumerate((pair_first, pair_second)):
            for c in range(CHUNKS):
                passes_on = far if step == 0 else near
                takes = near if step == 0 else far

                @pl.when(passes_on)
                def _():
                    wait_slot(par, fwd_slot, c)
                    fwd_copy(par, c).start()
                    wait_slot(par, 2 * pair + 1 - fwd_slot, c)

                @pl.when(takes)
                def _():
                    if step == 0:
                        wait_slot(par, sib_slot, c)
                    else:
                        wait_slot(par, pair, c)
                        wait_slot(par, pair + 1, c)

                if first:
                    for k in range(2):
                        for half in range(2):
                            local_load(c, pair + k, half).wait()
                if step == 0 and c == 0:
                    acc[...] = product(par, pair, c, slice(None))
                elif step == 0 or c < CHUNKS - 1:
                    acc[...] += product(par, pair, c, slice(None))
                else:
                    for o in range(CHUNKS):
                        cols = pl.ds(OFFSETS[o], WIDTHS[o])
                        psend[:, cols] = acc[:, cols] + product(par, pair, c, cols)
                        partial_copy(par, o).start()
                    for o in range(CHUNKS):
                        cols = pl.ds(piece + OFFSETS[o], WIDTHS[o])
                        acc[:, cols] += product(par, pair, c, cols)
        for c in range(CHUNKS):
            fwd_copy(par, c).wait_send()
            wait_own_sends(par, c)
        for o in range(CHUNKS):
            partial_copy(par, o).wait_recv()
            cols = pl.ds(OFFSETS[o], WIDTHS[o])
            combine(o, acc[:, pl.ds(piece + OFFSETS[o], WIDTHS[o])] + prec[par, :, cols])
        for o in range(CHUNKS):
            partial_copy(par, o).wait_send()

    center = c_ref[0]
    half_width = e_ref[0]

    def advance(t, par, first):
        other = 1 - par

        def combine(o, image):
            cols = pl.ds(OFFSETS[o], WIDTHS[o])
            shifted = image - center * state[par, :, cols]
            if first:
                following = shifted / half_width
            else:
                following = 2.0 * shifted / half_width - state[other, :, cols]
            state[other, :, cols] = following
            src[other, own_slot, :, cols] = following.astype(jnp.bfloat16)
            send_own(other, o)

        apply_matrix(t, par, first, combine)

    advance(0, 0, True)

    def step(t, carry):
        advance(t, lax.rem(t, 2), False)
        return carry

    lax.fori_loop(1, DEGREE, step, 0)

    y_copy = pltpu.make_async_copy(state.at[0], y_out, y_sem)
    y_copy.start()

    gall[me] = jnp.zeros_like(gall[me])

    def gram_part(o, image):
        cols = pl.ds(OFFSETS[o], WIDTHS[o])
        gall[me] += lax.dot_general(src[0, own_slot, :, cols], image.astype(jnp.bfloat16), (((1,), (1,)), ((), ())), preferred_element_type=jnp.float32)

    apply_matrix(DEGREE, 0, False, gram_part)

    def gram_copy(d):
        other = lax.rem(me + d, 8)
        return remote(gall.at[me], gall.at[me], gsend_sem.at[d], grecv_sem.at[me], (other // 2, lax.rem(other, 2)))

    for d in range(1, 8):
        gram_copy(d).start()
    for d in range(1, 8):
        origin = lax.rem(me + d, 8)
        remote(gall.at[origin], gall.at[origin], gsend_sem.at[d], grecv_sem.at[origin], (chip, core)).wait_recv()
    total = gall[0]
    for d in range(1, 8):
        total = total + gall[d]
    g_out[...] = total / (8 * piece)
    for d in range(1, 8):
        gram_copy(d).wait_send()
    y_copy.wait()


def solution(mesh):
    def local_filter(mat_tile, y_start, center, half_width):
        piece, width = y_start.shape
        rows, cols = mat_tile.shape
        y_t, gram = pl.pallas_call(
            functools.partial(filter_kernel, piece, width),
            out_shape=(jax.ShapeDtypeStruct((width, piece), jnp.float32), jax.ShapeDtypeStruct((width, width), jnp.float32)),
            in_specs=[
                pl.BlockSpec(memory_space=pl.ANY),
                pl.BlockSpec(memory_space=pl.ANY),
                pl.BlockSpec(memory_space=pltpu.SMEM),
                pl.BlockSpec(memory_space=pltpu.SMEM),
            ],
            out_specs=(pl.BlockSpec(memory_space=pl.ANY), pl.BlockSpec(memory_space=pltpu.VMEM)),
            scratch_shapes=[
                pltpu.VMEM((rows, cols), jnp.bfloat16),
                pltpu.VMEM((2, 5, width, piece), jnp.bfloat16),
                pltpu.VMEM((2, width, piece), jnp.float32),
                pltpu.VMEM((width, cols), jnp.float32),
                pltpu.VMEM((width, piece), jnp.float32),
                pltpu.VMEM((2, width, piece), jnp.float32),
                pltpu.VMEM((8, width, width), jnp.float32),
                pltpu.SemaphoreType.DMA((4, CHUNKS, 2)),
                pltpu.SemaphoreType.DMA((2, 4, CHUNKS)),
                pltpu.SemaphoreType.DMA((3, CHUNKS)),
                pltpu.SemaphoreType.DMA((CHUNKS,)),
                pltpu.SemaphoreType.DMA((CHUNKS,)),
                pltpu.SemaphoreType.DMA((2, CHUNKS)),
                pltpu.SemaphoreType.DMA((8,)),
                pltpu.SemaphoreType.DMA((8,)),
                pltpu.SemaphoreType.DMA,
            ],
            compiler_params=pltpu.CompilerParams(collective_id=0, has_side_effects=True, vmem_limit_bytes=56 * 1024 * 1024),
            name="filter",
        )(mat_tile, y_start.T, center.reshape(1), half_width.reshape(1))
        return y_t.T, gram

    return jax.shard_map(local_filter, mesh=mesh, in_specs=(P("row", "col"), P(("col", "row"), None), P(), P()), out_specs=(P(("col", "row"), None), P()), check_vma=False)
```

time: 545 us -> 123 us (0.23)
  waiting for transfers between devices: 231 us -> 0 us
  matrix products: 147 us -> 0 us
  blocking collectives: 134 us -> 0 us
  Pallas kernels: 0 us -> 118 us
  starting transfers between devices: 15 us -> 0 us
  between operations: 15.2 us -> 1.93 us
    reduce_scatter x9 -> x0, waiting for transfers between devices: 230 us -> none  [apply_matrix(): folded = lax.psum_scatter(part_sum, 'col', scatter_dimension=0, tiled=True)]
    dot_general x10 -> x0, matrix products: 147 us -> none  [the longest x9 146 us: apply_matrix(): part_sum = jnp.dot(mat_tile, src_block, preferred_element_type=jnp.float32)]
    pallas_call x0 -> x1, Pallas kernels: none -> 118 us  [local_filter(): pl.pallas_call(functools.partial(filter_kernel, piece, width), out_shape=...]
    all_gather x9 -> x0, blocking collectives: 101 us -> none  [apply_matrix(): src_block = lax.all_gather(y_low, 'row', axis=0, tiled=True)]
    psum x1 -> x0, blocking collectives: 32.8 us -> none  [local_filter(): gram_mat = lax.psum(local_gram, both_axes) / (mat_tile.shape[0] * row_count)]
    ppermute x9 -> x0, starting transfers between devices: 14.7 us -> none  [apply_matrix(): return lax.ppermute(folded, both_axes, realign_pairs)]
  transfers between devices with their start and end apart: 18 -> 0, of which waited for: 9 -> 0; matrix products, arithmetic and copies ran while one was open for 0% -> 0% of each run, Pallas kernels for 0% -> 0%
where the time goes in v1:
time: 123 us
  Pallas kernels  118 us (96%)
  local copies, waits for them, and re-layouts  3.12 us (3%)
  between operations  1.93 us (2%)
    pallas_call x1, Pallas kernels, local_filter(): pl.pallas_call(functools.partial(filter_kernel, piece, width), out_shape=...  118 us
    unnamed x2, local copies, waits for them, and re-layouts  3.12 us

profile of v1, /device:TPU:0, one launch (start us, length us, event | category | flops | bytes accessed | tf_op | source)
XLA Modules:
  0.0 123.2 jit_solution(3572739121431302129)
XLA Ops:
  1.9 118.2 %filter.1 = (f32[64,1408]{1,0:T(8,128)}, f32[64,64]{1,0:T(8,128)}) custom-call(bf16[5632,2816]{1,0:T(8,128)(2,1)} %a_ref.1, f32[64,1408]{1,0:T(8,128)} %bitcast.7, f32[1]{0:T(128)} %bitcast.4.c_ref, f32[1]{0:T(128)} %bitcast.5.e_ref), custom_call_target="tpu_custom_call" | custom-call | tf_op jit(solution)/shard_map/filter/pallas_call | solution.py:220
  120.1 1.7 %copy.10 = f32[1408,64]{0,1:T(8,128)} copy(f32[1408,64]{0,1:T(8,128)} %bitcast.6) | data formatting | bytes 720896
  121.9 1.4 %copy.11 = f32[64,64]{1,0:T(8,128)} copy(f32[64,64]{1,0:T(8,128)} %get-tuple-element.9) | data formatting | bytes 32768

commit v2 on v0

v2 whole, which is shorter than its diff:
```python
import functools

import jax
import jax.numpy as jnp
from jax import lax
from jax.experimental import pallas as pl
from jax.experimental.pallas import tpu as pltpu
from jax.sharding import PartitionSpec as P

DEGREE = 8
WIDTHS = (256, 512, 512, 128)
OFFSETS = (0, 256, 768, 1280)
CHUNKS = len(WIDTHS)
MESH = pl.DeviceIdType.MESH
EARLY, LATE = 0, 1


_held = []


def _push(rhs, staging_register, mxu_index, transpose=False):
    _held.append(rhs.T if transpose else rhs)


def _accl(acc, lhs, load_staged_rhs=None):
    acc[...] += jnp.dot(lhs, _held.pop(), preferred_element_type=jnp.float32)


def _pop(acc):
    value = acc[...]
    acc[...] = jnp.zeros_like(value)
    return value


def filter_kernel(piece, width, a_ref, y0_ref, c_ref, e_ref, y_out, g_out, tile, src, state, image, psend, prec, gall, tile_sem, recv_sem, send_sem, fwd_sem, psend_sem, prec_sem, gsend_sem, grecv_sem, y_sem):
    chip = lax.axis_index("col")
    core = lax.axis_index("row")
    me = chip * 2 + core
    sibling = 1 - core
    chip_bit = lax.rem(chip, 2)
    chip_x = chip + 1 - 2 * chip_bit
    chip_y = lax.rem(chip + 2, 4)
    group = chip // 2
    near_int = 1 - lax.abs(core - group)
    near = near_int == 1
    far = near_int == 0

    own_dest = 2 * chip_bit + core
    own_slot = near_int * own_dest + (1 - near_int) * 4
    pair_base = (2 * chip_bit, 2 * (1 - chip_bit))
    fwd_chip = near_int * chip_y + (1 - near_int) * chip_x

    def slot_of(step, kind):
        return pair_base[step] + (core if kind == LATE else sibling)

    def tile_load(step, kind, c, half):
        col = core if half else sibling
        rows = pl.ds(pl.multiple_of(slot_of(step, kind) * piece + OFFSETS[c], 128), WIDTHS[c])
        return pltpu.make_async_copy(
            a_ref.at[rows, pl.ds(pl.multiple_of(col * piece, 128), piece)],
            tile.at[rows, pl.ds(half * piece, piece)],
            tile_sem.at[step, kind, c, half],
        )

    def slot_view(par, slot, c):
        return src.at[par, slot, :, pl.ds(OFFSETS[c], WIDTHS[c])]

    def remote(src_view, dst_view, ssem, rsem, dev):
        return pltpu.make_async_remote_copy(src_ref=src_view, dst_ref=dst_view, send_sem=ssem, recv_sem=rsem, device_id=dev, device_id_type=MESH)

    def own_copy(par, c, d):
        dev = ((chip_x, group), (chip_y, group), (chip, group))[d]
        return remote(slot_view(par, own_slot, c), slot_view(par, own_dest, c), send_sem.at[d, c], recv_sem.at[par, own_dest, c], dev)

    def fwd_copy(par, step, kind, c):
        slot = slot_of(step, kind)
        return remote(slot_view(par, slot, c), slot_view(par, slot, c), fwd_sem.at[kind, c], recv_sem.at[par, slot, c], (fwd_chip, core))

    def wait_slot(par, slot, c):
        view = slot_view(par, slot, c)
        remote(view, view, fwd_sem.at[0, c], recv_sem.at[par, slot, c], (chip, core)).wait_recv()

    def partial_copy(par, o):
        cols = pl.ds(OFFSETS[o], WIDTHS[o])
        return remote(psend.at[:, cols], prec.at[par, :, cols], psend_sem.at[o], prec_sem.at[par, o], (chip, sibling))

    def send_own(par, c):
        own_copy(par, c, 0).start()
        own_copy(par, c, 1).start()

        @pl.when(far)
        def _():
            own_copy(par, c, 2).start()

    def wait_sends(par):
        for c in range(CHUNKS):
            own_copy(par, c, 0).wait_send()
            own_copy(par, c, 1).wait_send()

            @pl.when(far)
            def _():
                own_copy(par, c, 2).wait_send()

            for kind in (EARLY, LATE):

                @pl.when(near if (c + kind) % 2 == 0 else far)
                def _():
                    fwd_copy(par, 0, kind, c).wait_send()

    def arrive(par, step, kind, c):
        if step == 1:
            wait_slot(par, slot_of(1, kind), c)
            if (c + kind) % 2 == 0:

                @pl.when(near)
                def _():
                    fwd_copy(par, 1, kind, c).start()

            return

        if kind == EARLY:
            wait_slot(par, slot_of(0, kind), c)

        if kind == LATE or (c + kind) % 2 == 1:

            @pl.when(far)
            def _():
                if kind == LATE:
                    wait_slot(par, slot_of(0, kind), c)
                if (c + kind) % 2 == 1:
                    fwd_copy(par, 0, kind, c).start()

    y0_copy = pltpu.make_async_copy(y0_ref, state.at[0], y_sem)
    y0_copy.start()

    barrier = pltpu.get_barrier_semaphore()
    for d in range(1, 8):
        other = lax.rem(me + d, 8)
        pl.semaphore_signal(barrier, inc=1, device_id=(other // 2, lax.rem(other, 2)), device_id_type=MESH)

    for step in range(2):
        for kind in (EARLY, LATE):
            for c in range(CHUNKS):
                for half in range(2):
                    tile_load(step, kind, c, half).start()

    state[1] = jnp.zeros_like(state[1])
    y0_copy.wait()
    src[0, own_slot] = state[0].astype(jnp.bfloat16)
    pl.semaphore_wait(barrier, 7)
    for c in range(CHUNKS):
        send_own(0, c)
    center = c_ref[0]
    half_width = e_ref[0]

    def with_accumulators(accs0, accs1):
        for acc in accs0 + accs1:
            acc[...] = jnp.zeros_like(acc)

        def accumulate(par, halves, turn):
            lhs = jnp.concatenate([src[par, slot, :, pl.ds(off, 128)] for slot, off in halves], axis=1)
            for n in range(11):
                unit = n % 2 if n < 10 else turn % 2
                acc = (accs0, accs1)[unit][n // 2]
                parts = [tile[pl.ds(pl.multiple_of(slot * piece + off, 128), 128), pl.ds(256 * n, 256)] for slot, off in halves]
                reg = (n // 2 + turn) % 2
                _push(jnp.concatenate(parts, axis=0), staging_register=reg, mxu_index=unit)
                _accl(acc, lhs, load_staged_rhs=reg)

        def apply_matrix(par, first, combine):
            turn = 0
            for step in range(2):
                for kind in (EARLY, LATE):
                    slot = slot_of(step, kind)
                    for c in range(CHUNKS):
                        arrive(par, step, kind, c)
                        if first:
                            for half in range(2):
                                tile_load(step, kind, c, half).wait()
                        if c < CHUNKS - 1:
                            for k in range(WIDTHS[c] // 256):
                                off = OFFSETS[c] + 256 * k
                                accumulate(par, ((slot, off), (slot, off + 128)), turn)
                                turn += 1
                accumulate(par, ((slot_of(step, EARLY), OFFSETS[-1]), (slot_of(step, LATE), OFFSETS[-1])), turn)
                turn += 1
            for n in range(5):
                psend[:, pl.ds(256 * n, 256)] = _pop((accs0, accs1)[n % 2][n // 2])
            middle = _pop(accs1[2])
            psend[:, pl.ds(1280, 128)] = middle[:, :128]
            for o in range(CHUNKS):
                partial_copy(par, o).start()
            image[:, pl.ds(0, 128)] = middle[:, 128:]
            for n in range(6, 10):
                image[:, pl.ds(256 * n - piece, 256)] = _pop((accs0, accs1)[n % 2][n // 2])
            image[:, pl.ds(1152, 256)] = _pop(accs0[5]) + _pop(accs1[5])
            wait_sends(par)
            for o in range(CHUNKS):
                partial_copy(par, o).wait_recv()
                cols = pl.ds(OFFSETS[o], WIDTHS[o])
                combine(o, image[:, cols] + prec[par, :, cols])
            for o in range(CHUNKS):
                partial_copy(par, o).wait_send()

        def advance(par, first):
            other = 1 - par

            def combine(o, total):
                cols = pl.ds(OFFSETS[o], WIDTHS[o])
                shifted = total - center * state[par, :, cols]
                if first:
                    following = shifted / half_width
                else:
                    following = 2.0 * shifted / half_width - state[other, :, cols]
                state[other, :, cols] = following
                src[other, own_slot, :, cols] = following.astype(jnp.bfloat16)
                send_own(other, o)

            apply_matrix(par, first, combine)

        advance(0, True)

        def step(t, carry):
            advance(lax.rem(t, 2), False)
            return carry

        lax.fori_loop(1, DEGREE, step, 0)

        y_copy = pltpu.make_async_copy(state.at[0], y_out, y_sem)
        y_copy.start()

        def gram_part(o, total):
            low = total.astype(jnp.bfloat16)
            for k in range(max(WIDTHS[o] // 256, 1)):
                size = min(WIDTHS[o], 256)
                left = src[0, own_slot, :, pl.ds(OFFSETS[o] + 256 * k, size)]
                right = low[:, 256 * k : 256 * k + size]
                if size < 256:
                    left = jnp.concatenate([left, jnp.zeros_like(left)], axis=1)
                    right = jnp.concatenate([right, jnp.zeros_like(right)], axis=1)
                right = jnp.concatenate([right, jnp.zeros((256 - width, 256), jnp.bfloat16)], axis=0)
                unit = (o + k) % 2
                _push(right, staging_register=0, mxu_index=unit, transpose=True)
                _accl((accs0, accs1)[unit][0], left, load_staged_rhs=0)

        apply_matrix(0, False, gram_part)
        gall[me] = (_pop(accs0[0]) + _pop(accs1[0]))[:, :width]

        def gram_copy(d):
            other = lax.rem(me + d, 8)
            return remote(gall.at[me], gall.at[me], gsend_sem.at[d], grecv_sem.at[me], (other // 2, lax.rem(other, 2)))

        for d in range(1, 8):
            gram_copy(d).start()
        for d in range(1, 8):
            origin = lax.rem(me + d, 8)
            remote(gall.at[origin], gall.at[origin], gsend_sem.at[d], grecv_sem.at[origin], (chip, core)).wait_recv()
        total = gall[0]
        for d in range(1, 8):
            total = total + gall[d]
        g_out[...] = total / (8 * piece)
        for d in range(1, 8):
            gram_copy(d).wait_send()
        y_copy.wait()

    accs = [tuple(pltpu.VMEM((width, 256), jnp.float32) for _ in range(6)) for unit in range(2)]
    pl.run_scoped(with_accumulators, *accs)


def solution(mesh):
    def local_filter(mat_tile, y_start, center, half_width):
        piece, width = y_start.shape
        rows, cols = mat_tile.shape
        y_t, gram = pl.pallas_call(
            functools.partial(filter_kernel, piece, width),
            out_shape=(jax.ShapeDtypeStruct((width, piece), jnp.float32), jax.ShapeDtypeStruct((width, width), jnp.float32)),
            in_specs=[pl.BlockSpec(memory_space=pl.ANY)] * 2 + [pl.BlockSpec(memory_space=pltpu.SMEM)] * 2,
            out_specs=(pl.BlockSpec(memory_space=pl.ANY), pl.BlockSpec(memory_space=pltpu.VMEM)),
            scratch_shapes=[
                pltpu.VMEM((rows, cols), jnp.bfloat16),
                pltpu.VMEM((2, 5, width, piece), jnp.bfloat16),
                pltpu.VMEM((2, width, piece), jnp.float32),
                pltpu.VMEM((width, piece), jnp.float32),
                pltpu.VMEM((width, piece), jnp.float32),
                pltpu.VMEM((2, width, piece), jnp.float32),
                pltpu.VMEM((8, width, width), jnp.float32),
                pltpu.SemaphoreType.DMA((2, 2, CHUNKS, 2)),
                pltpu.SemaphoreType.DMA((2, 4, CHUNKS)),
                pltpu.SemaphoreType.DMA((3, CHUNKS)),
                pltpu.SemaphoreType.DMA((2, CHUNKS)),
                pltpu.SemaphoreType.DMA((CHUNKS,)),
                pltpu.SemaphoreType.DMA((2, CHUNKS)),
                pltpu.SemaphoreType.DMA((8,)),
                pltpu.SemaphoreType.DMA((8,)),
                pltpu.SemaphoreType.DMA,
            ],
            compiler_params=pltpu.CompilerParams(collective_id=0, has_side_effects=True, vmem_limit_bytes=56 * 1024 * 1024),
            name="filter",
        )(mat_tile, y_start.T, center.reshape(1), half_width.reshape(1))
        return y_t.T, gram

    return jax.shard_map(local_filter, mesh=mesh, in_specs=(P("row", "col"), P(("col", "row"), None), P(), P()), out_specs=(P(("col", "row"), None), P()), check_vma=False)
```

time: 545 us -> 112 us (0.21)
  waiting for transfers between devices: 231 us -> 0 us
  matrix products: 147 us -> 0 us
  blocking collectives: 134 us -> 0 us
  Pallas kernels: 0 us -> 107 us
  starting transfers between devices: 15 us -> 0 us
  between operations: 15.2 us -> 1.93 us
    reduce_scatter x9 -> x0, waiting for transfers between devices: 230 us -> none  [apply_matrix(): folded = lax.psum_scatter(part_sum, 'col', scatter_dimension=0, tiled=True)]
    dot_general x10 -> x0, matrix products: 147 us -> none  [the longest x9 146 us: apply_matrix(): part_sum = jnp.dot(mat_tile, src_block, preferred_element_type=jnp.float32)]
    pallas_call x0 -> x1, Pallas kernels: none -> 107 us  [local_filter(): pl.pallas_call(functools.partial(filter_kernel, piece, width), out_shape=...]
    all_gather x9 -> x0, blocking collectives: 101 us -> none  [apply_matrix(): src_block = lax.all_gather(y_low, 'row', axis=0, tiled=True)]
    psum x1 -> x0, blocking collectives: 32.8 us -> none  [local_filter(): gram_mat = lax.psum(local_gram, both_axes) / (mat_tile.shape[0] * row_count)]
    ppermute x9 -> x0, starting transfers between devices: 14.7 us -> none  [apply_matrix(): return lax.ppermute(folded, both_axes, realign_pairs)]
  transfers between devices with their start and end apart: 18 -> 0, of which waited for: 9 -> 0; matrix products, arithmetic and copies ran while one was open for 0% -> 0% of each run, Pallas kernels for 0% -> 0%
where the time goes in v2:
time: 112 us
  Pallas kernels  107 us (96%)
  local copies, waits for them, and re-layouts  3.12 us (3%)
  between operations  1.93 us (2%)
    pallas_call x1, Pallas kernels, local_filter(): pl.pallas_call(functools.partial(filter_kernel, piece, width), out_shape=...  107 us
    unnamed x2, local copies, waits for them, and re-layouts  3.12 us

profile of v2, /device:TPU:0, one launch (start us, length us, event | category | flops | bytes accessed | tf_op | source)
XLA Modules:
  0.0 112.2 jit_solution(6716875338759564686)
XLA Ops:
  1.9 107.2 %filter.1 = (f32[64,1408]{1,0:T(8,128)}, f32[64,64]{1,0:T(8,128)}) custom-call(bf16[5632,2816]{1,0:T(8,128)(2,1)} %a_ref.1, f32[64,1408]{1,0:T(8,128)} %bitcast.7, f32[1]{0:T(128)} %bitcast.4.c_ref, f32[1]{0:T(128)} %bitcast.5.e_ref), custom_call_target="tpu_custom_call" | custom-call | tf_op jit(solution)/shard_map/filter/pallas_call | solution.py:274
  109.1 1.7 %copy.10 = f32[1408,64]{0,1:T(8,128)} copy(f32[1408,64]{0,1:T(8,128)} %bitcast.6) | data formatting | bytes 720896
  110.8 1.4 %copy.11 = f32[64,64]{1,0:T(8,128)} copy(f32[64,64]{1,0:T(8,128)} %get-tuple-element.9) | data formatting | bytes 32768

commit v3 on v2

v3 whole, which is shorter than its diff:
```python
import functools

import jax
import jax.numpy as jnp
from jax import lax
from jax.experimental import pallas as pl
from jax.experimental.pallas import tpu as pltpu
from jax.sharding import PartitionSpec as P

DEGREE = 8
WIDTHS = (256, 512, 512, 128)
OFFSETS = (0, 256, 768, 1280)
CHUNKS = len(WIDTHS)
BLOCKS = ((0, 1), (2, 3))
FINAL_BLOCKS = ((0, 1), (2,), (3,))
MESH = pl.DeviceIdType.MESH
EARLY, LATE = 0, 1


def filter_kernel(piece, width, a_ref, y0_ref, c_ref, e_ref, y_out, g_out, tile, src, state, acc, psend, prec, gall, tile_sem, recv_sem, send_sem, fwd_sem, psend_sem, prec_sem, gsend_sem, grecv_sem, y_sem):
    chip = lax.axis_index("col")
    core = lax.axis_index("row")
    me = chip * 2 + core
    sibling = 1 - core
    chip_bit = lax.rem(chip, 2)
    chip_x = chip + 1 - 2 * chip_bit
    chip_y = lax.rem(chip + 2, 4)
    group = chip // 2
    near_int = 1 - lax.abs(core - group)
    near = near_int == 1
    far = near_int == 0

    own_dest = 2 * chip_bit + core
    own_slot = near_int * own_dest + (1 - near_int) * 4
    pair_base = (2 * chip_bit, 2 * (1 - chip_bit))
    fwd_chip = near_int * chip_y + (1 - near_int) * chip_x

    def slot_of(step, kind):
        return pair_base[step] + (core if kind == LATE else sibling)

    def tile_load(step, kind, c, half):
        col = core if half else sibling
        rows = pl.ds(pl.multiple_of(slot_of(step, kind) * piece + OFFSETS[c], 128), WIDTHS[c])
        return pltpu.make_async_copy(
            a_ref.at[rows, pl.ds(pl.multiple_of(col * piece, 128), piece)],
            tile.at[rows, pl.ds(half * piece, piece)],
            tile_sem.at[step, kind, c, half],
        )

    def slot_view(par, slot, c):
        return src.at[par, slot, :, pl.ds(OFFSETS[c], WIDTHS[c])]

    def remote(src_view, dst_view, ssem, rsem, dev):
        return pltpu.make_async_remote_copy(src_ref=src_view, dst_ref=dst_view, send_sem=ssem, recv_sem=rsem, device_id=dev, device_id_type=MESH)

    def own_copy(par, c, d):
        dev = ((chip_x, group), (chip_y, group), (chip, group))[d]
        return remote(slot_view(par, own_slot, c), slot_view(par, own_dest, c), send_sem.at[d, c], recv_sem.at[par, own_dest, c], dev)

    def fwd_copy(par, step, kind, c):
        slot = slot_of(step, kind)
        return remote(slot_view(par, slot, c), slot_view(par, slot, c), fwd_sem.at[kind, c], recv_sem.at[par, slot, c], (fwd_chip, core))

    def wait_slot(par, slot, c):
        view = slot_view(par, slot, c)
        remote(view, view, fwd_sem.at[0, c], recv_sem.at[par, slot, c], (chip, core)).wait_recv()

    def partial_copy(par, o):
        cols = pl.ds(OFFSETS[o], WIDTHS[o])
        return remote(psend.at[:, cols], prec.at[par, :, cols], psend_sem.at[o], prec_sem.at[par, o], (chip, sibling))

    def send_own(par, c):
        own_copy(par, c, 0).start()
        own_copy(par, c, 1).start()

        @pl.when(far)
        def _():
            own_copy(par, c, 2).start()

    def wait_sends(par):
        for c in range(CHUNKS):
            own_copy(par, c, 0).wait_send()
            own_copy(par, c, 1).wait_send()

            @pl.when(far)
            def _():
                own_copy(par, c, 2).wait_send()

            for kind in (EARLY, LATE):

                @pl.when(near if (c + kind) % 2 == 0 else far)
                def _():
                    fwd_copy(par, 0, kind, c).wait_send()

    def arrive(par, step, kind, c):
        if step == 1:
            wait_slot(par, slot_of(1, kind), c)
            if (c + kind) % 2 == 0:

                @pl.when(near)
                def _():
                    fwd_copy(par, 1, kind, c).start()

            return

        if kind == EARLY:
            wait_slot(par, slot_of(0, kind), c)

        if kind == LATE or (c + kind) % 2 == 1:

            @pl.when(far)
            def _():
                if kind == LATE:
                    wait_slot(par, slot_of(0, kind), c)
                if (c + kind) % 2 == 1:
                    fwd_copy(par, 0, kind, c).start()

    y0_copy = pltpu.make_async_copy(y0_ref, state.at[0], y_sem)
    y0_copy.start()

    barrier = pltpu.get_barrier_semaphore()
    for d in range(1, 8):
        other = lax.rem(me + d, 8)
        pl.semaphore_signal(barrier, inc=1, device_id=(other // 2, lax.rem(other, 2)), device_id_type=MESH)

    for step in range(2):
        for kind in (EARLY, LATE):
            for c in range(CHUNKS):
                for half in range(2):
                    tile_load(step, kind, c, half).start()

    state[1] = jnp.zeros_like(state[1])
    acc[...] = jnp.zeros_like(acc)
    y0_copy.wait()
    src[0, own_slot] = state[0].astype(jnp.bfloat16)
    pl.semaphore_wait(barrier, 7)
    for c in range(CHUNKS):
        send_own(0, c)
    center = c_ref[()]
    half_width = e_ref[()]

    def product(par, slot, off, size, cols):
        rows = pl.ds(pl.multiple_of(slot * piece + off, 128), size)
        return jnp.dot(src[par, slot, :, pl.ds(off, size)], tile[rows, cols], preferred_element_type=jnp.float32)

    def apply_matrix(par, first, combine):
        for step in range(2):
            for kind in (EARLY, LATE):
                slot = slot_of(step, kind)
                final = step == 1 and kind == LATE
                for block in FINAL_BLOCKS if final else BLOCKS:
                    for c in block:
                        arrive(par, step, kind, c)
                        if first:
                            for half in range(2):
                                tile_load(step, kind, c, half).wait()
                    off, size = OFFSETS[block[0]], sum(WIDTHS[c] for c in block)
                    if final and block[0] == CHUNKS - 1:
                        psend[...] = acc[:, :piece] + product(par, slot, off, size, pl.ds(0, piece))
                        acc[:, piece:] += product(par, slot, off, size, pl.ds(piece, piece))
                    else:
                        acc[...] += product(par, slot, off, size, slice(None))
        for o in range(CHUNKS):
            partial_copy(par, o).start()
        wait_sends(par)
        for o in range(CHUNKS):
            partial_copy(par, o).wait_recv()
            combine(o, acc[:, pl.ds(piece + OFFSETS[o], WIDTHS[o])] + prec[par, :, pl.ds(OFFSETS[o], WIDTHS[o])])
        acc[...] = jnp.zeros_like(acc)
        for o in range(CHUNKS):
            partial_copy(par, o).wait_send()

    def advance(par, first):
        other = 1 - par

        def combine(o, total):
            cols = pl.ds(OFFSETS[o], WIDTHS[o])
            shifted = total - center * state[par, :, cols]
            if first:
                following = shifted / half_width
            else:
                following = 2.0 * shifted / half_width - state[other, :, cols]
            state[other, :, cols] = following
            src[other, own_slot, :, cols] = following.astype(jnp.bfloat16)
            send_own(other, o)

        apply_matrix(par, first, combine)

    advance(0, True)

    def step(t, carry):
        advance(lax.rem(t, 2), False)
        return carry

    lax.fori_loop(1, DEGREE, step, 0)

    y_out[...] = state[0]
    gall[me] = jnp.zeros_like(gall[me])

    def gram_part(o, total):
        cols = pl.ds(OFFSETS[o], WIDTHS[o])
        gall[me] += lax.dot_general(src[0, own_slot, :, cols], total.astype(jnp.bfloat16), (((1,), (1,)), ((), ())), preferred_element_type=jnp.float32)

    apply_matrix(0, False, gram_part)

    def gram_copy(d):
        other = lax.rem(me + d, 8)
        return remote(gall.at[me], gall.at[me], gsend_sem.at[d], grecv_sem.at[me], (other // 2, lax.rem(other, 2)))

    for d in range(1, 8):
        gram_copy(d).start()
    for d in range(1, 8):
        origin = lax.rem(me + d, 8)
        remote(gall.at[origin], gall.at[origin], gsend_sem.at[d], grecv_sem.at[origin], (chip, core)).wait_recv()
    total = gall[0]
    for d in range(1, 8):
        total = total + gall[d]
    g_out[...] = total / (8 * piece)
    for d in range(1, 8):
        gram_copy(d).wait_send()


def solution(mesh):
    def local_filter(mat_tile, y_start, center, half_width):
        piece, width = y_start.shape
        rows, cols = mat_tile.shape
        y_t, gram = pl.pallas_call(
            functools.partial(filter_kernel, piece, width),
            out_shape=(pltpu.VMEM((width, piece), jnp.float32), pltpu.VMEM((width, width), jnp.float32)),
            in_specs=[pl.BlockSpec(memory_space=pl.ANY)] * 2 + [pl.BlockSpec(memory_space=pltpu.SMEM)] * 2,
            out_specs=(pl.BlockSpec(memory_space=pltpu.VMEM),) * 2,
            scratch_shapes=[
                pltpu.VMEM((rows, cols), jnp.bfloat16),
                pltpu.VMEM((2, 5, width, piece), jnp.bfloat16),
                pltpu.VMEM((2, width, piece), jnp.float32),
                pltpu.VMEM((width, cols), jnp.float32),
                pltpu.VMEM((width, piece), jnp.float32),
                pltpu.VMEM((2, width, piece), jnp.float32),
                pltpu.VMEM((8, width, width), jnp.float32),
                pltpu.SemaphoreType.DMA((2, 2, CHUNKS, 2)),
                pltpu.SemaphoreType.DMA((2, 4, CHUNKS)),
                pltpu.SemaphoreType.DMA((3, CHUNKS)),
                pltpu.SemaphoreType.DMA((2, CHUNKS)),
                pltpu.SemaphoreType.DMA((CHUNKS,)),
                pltpu.SemaphoreType.DMA((2, CHUNKS)),
                pltpu.SemaphoreType.DMA((8,)),
                pltpu.SemaphoreType.DMA((8,)),
                pltpu.SemaphoreType.DMA,
            ],
            compiler_params=pltpu.CompilerParams(collective_id=0, has_side_effects=True, vmem_limit_bytes=56 * 1024 * 1024),
            name="filter",
        )(mat_tile, y_start.T, center, half_width)
        return y_t.T, gram

    return jax.shard_map(local_filter, mesh=mesh, in_specs=(P("row", "col"), P(("col", "row"), None), P(), P()), out_specs=(P(("col", "row"), None), P()), check_vma=False)
```

time: 112 us -> 110 us (0.982)
  local copies, waits for them, and re-layouts: 3.12 us -> 1.35 us
    unnamed x2, local copies, waits for them, and re-layouts: 3.12 us -> 1.35 us
where the time goes in v3:
time: 110 us
  Pallas kernels  107 us (97%)
  between operations  1.93 us (2%)
  local copies, waits for them, and re-layouts  1.35 us (1%)
    pallas_call x1, Pallas kernels, local_filter(): pl.pallas_call(functools.partial(filter_kernel, piece, width), out_shape=...  107 us

profile of v3, /device:TPU:0, one launch (start us, length us, event | category | flops | bytes accessed | tf_op | source)
XLA Modules:
  0.0 110.3 jit_solution(3000677224125607265)
XLA Ops:
  1.9 107.0 %filter.1 = (f32[64,1408]{1,0:T(8,128)S(1)}, f32[64,64]{1,0:T(8,128)S(1)}) custom-call(bf16[5632,2816]{1,0:T(8,128)(2,1)} %a_ref.1, f32[64,1408]{1,0:T(8,128)} %bitcast.3, f32[]{:T(128)S(6)} %copy.10.c_ref, f32[]{:T(128)S(6)} %copy.11.e_ref), custom_call_target="tpu_custom_call" | custom-call | tf_op jit(solution)/shard_map/filter/pallas_call | solution.py:227
  109.0 0.7 copy.8
  109.7 0.6 copy.9

commit v4 on v3

--- a/solution.py
+++ b/solution.py
@@ -8,16 +8,18 @@
 from jax.sharding import PartitionSpec as P
 
 DEGREE = 8
-WIDTHS = (256, 512, 512, 128)
-OFFSETS = (0, 256, 768, 1280)
+WIDTHS = (256, 256, 256, 256, 256, 128)
+OFFSETS = (0, 256, 512, 768, 1024, 1280)
 CHUNKS = len(WIDTHS)
-BLOCKS = ((0, 1), (2, 3))
-FINAL_BLOCKS = ((0, 1), (2,), (3,))
 MESH = pl.DeviceIdType.MESH
 EARLY, LATE = 0, 1
-
-
-def filter_kernel(piece, width, a_ref, y0_ref, c_ref, e_ref, y_out, g_out, tile, src, state, acc, psend, prec, gall, tile_sem, recv_sem, send_sem, fwd_sem, psend_sem, prec_sem, gsend_sem, grecv_sem, y_sem):
+BLOCKS = (
+    (((EARLY, 0, 0),), ((EARLY, 1, 2),), ((LATE, 0, 0), (EARLY, 3, 3)), ((LATE, 1, 1), (EARLY, 4, 5)), ((LATE, 2, 3),), ((LATE, 4, 5),)),
+    (((EARLY, 0, 1),), ((EARLY, 2, 3), (LATE, 0, 0)), ((LATE, 1, 1), (EARLY, 4, 5), (LATE, 2, 2)), ((LATE, 3, 5),)),
+)
+
+
+def filter_kernel(piece, width, a_ref, y0_ref, c_ref, e_ref, y_out, g_out, tile, src, state, acc, prec, gall, image, tile_sem, recv_sem, send_sem, fwd_sem, psend_sem, prec_sem, gsend_sem, grecv_sem, y_sem):
     chip = lax.axis_index("col")
     core = lax.axis_index("row")
     me = chip * 2 + core
@@ -67,7 +69,7 @@
 
     def partial_copy(par, o):
         cols = pl.ds(OFFSETS[o], WIDTHS[o])
-        return remote(psend.at[:, cols], prec.at[par, :, cols], psend_sem.at[o], prec_sem.at[par, o], (chip, sibling))
+        return remote(acc.at[:, cols], prec.at[par, :, cols], psend_sem.at[o], prec_sem.at[par, o], (chip, sibling))
 
     def send_own(par, c):
         own_copy(par, c, 0).start()
@@ -130,7 +132,6 @@
                     tile_load(step, kind, c, half).start()
 
     state[1] = jnp.zeros_like(state[1])
-    acc[...] = jnp.zeros_like(acc)
     y0_copy.wait()
     src[0, own_slot] = state[0].astype(jnp.bfloat16)
     pl.semaphore_wait(barrier, 7)
@@ -145,28 +146,28 @@
 
     def apply_matrix(par, first, combine):
         for step in range(2):
-            for kind in (EARLY, LATE):
-                slot = slot_of(step, kind)
-                final = step == 1 and kind == LATE
-                for block in FINAL_BLOCKS if final else BLOCKS:
-                    for c in block:
+            for index, block in enumerate(BLOCKS[step]):
+                for kind, low, high in block:
+                    for c in range(low, high + 1):
                         arrive(par, step, kind, c)
                         if first:
                             for half in range(2):
                                 tile_load(step, kind, c, half).wait()
-                    off, size = OFFSETS[block[0]], sum(WIDTHS[c] for c in block)
-                    if final and block[0] == CHUNKS - 1:
-                        psend[...] = acc[:, :piece] + product(par, slot, off, size, pl.ds(0, piece))
-                        acc[:, piece:] += product(par, slot, off, size, pl.ds(piece, piece))
-                    else:
-                        acc[...] += product(par, slot, off, size, slice(None))
+
+                def total(cols):
+                    parts = [product(par, slot_of(step, kind), OFFSETS[low], OFFSETS[high] + WIDTHS[high] - OFFSETS[low], cols) for kind, low, high in block]
+                    return sum(parts[1:], parts[0])
+
+                if step == 0 and index == 0:
+                    acc[...] = total(slice(None))
+                else:
+                    acc[...] += total(slice(None))
         for o in range(CHUNKS):
             partial_copy(par, o).start()
         wait_sends(par)
         for o in range(CHUNKS):
             partial_copy(par, o).wait_recv()
             combine(o, acc[:, pl.ds(piece + OFFSETS[o], WIDTHS[o])] + prec[par, :, pl.ds(OFFSETS[o], WIDTHS[o])])
-        acc[...] = jnp.zeros_like(acc)
         for o in range(CHUNKS):
             partial_copy(par, o).wait_send()
 
@@ -195,13 +196,14 @@
     lax.fori_loop(1, DEGREE, step, 0)
 
     y_out[...] = state[0]
-    gall[me] = jnp.zeros_like(gall[me])
 
     def gram_part(o, total):
-        cols = pl.ds(OFFSETS[o], WIDTHS[o])
-        gall[me] += lax.dot_general(src[0, own_slot, :, cols], total.astype(jnp.bfloat16), (((1,), (1,)), ((), ())), preferred_element_type=jnp.float32)
+        image[:, pl.ds(OFFSETS[o], WIDTHS[o])] = total.astype(jnp.bfloat16)
 
     apply_matrix(0, False, gram_part)
+    gram_part_sum = lax.dot_general(src[0, own_slot], image[...], (((1,), (1,)), ((), ())), preferred_element_type=jnp.float32)
+    half = width // 2
+    gall[me] = jnp.concatenate([gram_part_sum[:half], gram_part_sum[half:]], axis=1)
 
     def gram_copy(d):
         other = lax.rem(me + d, 8)
@@ -215,7 +217,9 @@
     total = gall[0]
     for d in range(1, 8):
         total = total + gall[d]
-    g_out[...] = total / (8 * piece)
+    total = total / (8 * piece)
+    g_out[:half] = total[:, :width]
+    g_out[half:] = total[:, width:]
     for d in range(1, 8):
         gram_copy(d).wait_send()
 
@@ -234,9 +238,9 @@
                 pltpu.VMEM((2, 5, width, piece), jnp.bfloat16),
                 pltpu.VMEM((2, width, piece), jnp.float32),
                 pltpu.VMEM((width, cols), jnp.float32),
-                pltpu.VMEM((width, piece), jnp.float32),
                 pltpu.VMEM((2, width, piece), jnp.float32),
-                pltpu.VMEM((8, width, width), jnp.float32),
+                pltpu.VMEM((8, width // 2, 2 * width), jnp.float32),
+                pltpu.VMEM((width, piece), jnp.bfloat16),
                 pltpu.SemaphoreType.DMA((2, 2, CHUNKS, 2)),
                 pltpu.SemaphoreType.DMA((2, 4, CHUNKS)),
                 pltpu.SemaphoreType.DMA((3, CHUNKS)),

time: 110 us -> 109 us (level)
  Pallas kernels: 107 us -> 105 us
    pallas_call x1, Pallas kernels: 107 us -> 105 us  [local_filter(): pl.pallas_call(functools.partial(filter_kernel, piece, width), out_shape=...]
where the time goes in v4:
time: 109 us; the launch traced here: 108 us
  Pallas kernels  105 us (96%)
  between operations  1.93 us (2%)
  local copies, waits for them, and re-layouts  1.35 us (1%)
    pallas_call x1, Pallas kernels, local_filter(): pl.pallas_call(functools.partial(filter_kernel, piece, width), out_shape=...  105 us

profile of v4, /device:TPU:0, one launch (start us, length us, event | category | flops | bytes accessed | tf_op | source)
XLA Modules:
  0.0 108.5 jit_solution(3610653034480794899)
XLA Ops:
  1.9 105.2 %filter.1 = (f32[64,1408]{1,0:T(8,128)S(1)}, f32[64,64]{1,0:T(8,128)S(1)}) custom-call(bf16[5632,2816]{1,0:T(8,128)(2,1)} %a_ref.1, f32[64,1408]{1,0:T(8,128)} %bitcast.3, f32[]{:T(128)S(6)} %copy.10.c_ref, f32[]{:T(128)S(6)} %copy.11.e_ref), custom_call_target="tpu_custom_call" | custom-call | tf_op jit(solution)/shard_map/filter/pallas_call | solution.py:231
  107.1 0.7 copy.8
  107.8 0.6 copy.9

commit v5 on v4

--- a/solution.py
+++ b/solution.py
@@ -14,9 +14,10 @@
 MESH = pl.DeviceIdType.MESH
 EARLY, LATE = 0, 1
 BLOCKS = (
-    (((EARLY, 0, 0),), ((EARLY, 1, 2),), ((LATE, 0, 0), (EARLY, 3, 3)), ((LATE, 1, 1), (EARLY, 4, 5)), ((LATE, 2, 3),), ((LATE, 4, 5),)),
-    (((EARLY, 0, 1),), ((EARLY, 2, 3), (LATE, 0, 0)), ((LATE, 1, 1), (EARLY, 4, 5), (LATE, 2, 2)), ((LATE, 3, 5),)),
+    (((EARLY, 0, 0),), ((EARLY, 1, 2),), ((EARLY, 3, 3), (LATE, 0, 0)), ((LATE, 1, 1), (EARLY, 4, 4)), ((EARLY, 5, 5), (LATE, 2, 3)), ((LATE, 4, 5),)),
+    (((EARLY, 1, 1), (EARLY, 3, 3), (LATE, 0, 0)), ((EARLY, 5, 5), (LATE, 2, 2), (LATE, 4, 4)), ((EARLY, 0, 0), (EARLY, 2, 2), (LATE, 1, 1)), ((EARLY, 4, 4), (LATE, 3, 3)), ((LATE, 5, 5),)),
 )
+PASSED = (((EARLY, 0), (EARLY, 2), (LATE, 1)), ((EARLY, 4), (LATE, 3)), ((LATE, 5),), (), ())
 
 
 def filter_kernel(piece, width, a_ref, y0_ref, c_ref, e_ref, y_out, g_out, tile, src, state, acc, prec, gall, image, tile_sem, recv_sem, send_sem, fwd_sem, psend_sem, prec_sem, gsend_sem, grecv_sem, y_sem):
@@ -96,13 +97,14 @@
 
     def arrive(par, step, kind, c):
         if step == 1:
-            wait_slot(par, slot_of(1, kind), c)
             if (c + kind) % 2 == 0:
 
-                @pl.when(near)
+                @pl.when(far)
                 def _():
-                    fwd_copy(par, 1, kind, c).start()
-
+                    wait_slot(par, slot_of(1, kind), c)
+
+            else:
+                wait_slot(par, slot_of(1, kind), c)
             return
 
         if kind == EARLY:
@@ -120,6 +122,8 @@
     y0_copy = pltpu.make_async_copy(y0_ref, state.at[0], y_sem)
     y0_copy.start()
 
+    padding = pl.ds(2 * piece, acc.shape[1] - 2 * piece)
+    tile[:, padding] = jnp.zeros_like(tile[:, padding])
     barrier = pltpu.get_barrier_semaphore()
     for d in range(1, 8):
         other = lax.rem(me + d, 8)
@@ -147,6 +151,14 @@
     def apply_matrix(par, first, combine):
         for step in range(2):
             for index, block in enumerate(BLOCKS[step]):
+                if step == 1 and PASSED[index]:
+
+                    @pl.when(near)
+                    def _():
+                        for kind, c in PASSED[index]:
+                            wait_slot(par, slot_of(1, kind), c)
+                            fwd_copy(par, 1, kind, c).start()
+
                 for kind, low, high in block:
                     for c in range(low, high + 1):
                         arrive(par, step, kind, c)
@@ -228,16 +240,17 @@
     def local_filter(mat_tile, y_start, center, half_width):
         piece, width = y_start.shape
         rows, cols = mat_tile.shape
+        padded = -(-cols // 512) * 512
         y_t, gram = pl.pallas_call(
             functools.partial(filter_kernel, piece, width),
             out_shape=(pltpu.VMEM((width, piece), jnp.float32), pltpu.VMEM((width, width), jnp.float32)),
             in_specs=[pl.BlockSpec(memory_space=pl.ANY)] * 2 + [pl.BlockSpec(memory_space=pltpu.SMEM)] * 2,
             out_specs=(pl.BlockSpec(memory_space=pltpu.VMEM),) * 2,
             scratch_shapes=[
-                pltpu.VMEM((rows, cols), jnp.bfloat16),
+                pltpu.VMEM((rows, padded), jnp.bfloat16),
                 pltpu.VMEM((2, 5, width, piece), jnp.bfloat16),
                 pltpu.VMEM((2, width, piece), jnp.float32),
-                pltpu.VMEM((width, cols), jnp.float32),
+                pltpu.VMEM((width, padded), jnp.float32),
                 pltpu.VMEM((2, width, piece), jnp.float32),
                 pltpu.VMEM((8, width // 2, 2 * width), jnp.float32),
                 pltpu.VMEM((width, piece), jnp.bfloat16),

time: 109 us -> 116 us (1.064)
  Pallas kernels: 105 us -> 113 us
    pallas_call x1, Pallas kernels: 105 us -> 113 us  [local_filter(): pl.pallas_call(functools.partial(filter_kernel, piece, width), out_shape=...]
where the time goes in v5:
time: 116 us
  Pallas kernels  113 us (97%)
  between operations  1.93 us (2%)
  local copies, waits for them, and re-layouts  1.35 us (1%)
    pallas_call x1, Pallas kernels, local_filter(): pl.pallas_call(functools.partial(filter_kernel, piece, width), out_shape=...  113 us

profile of v5, /device:TPU:0, one launch (start us, length us, event | category | flops | bytes accessed | tf_op | source)
XLA Modules:
  0.0 115.9 jit_solution(16656187127523380969)
XLA Ops:
  1.9 112.7 %filter.1 = (f32[64,1408]{1,0:T(8,128)S(1)}, f32[64,64]{1,0:T(8,128)S(1)}) custom-call(bf16[5632,2816]{1,0:T(8,128)(2,1)} %a_ref.1, f32[64,1408]{1,0:T(8,128)} %bitcast.3, f32[]{:T(128)S(6)} %copy.10.c_ref, f32[]{:T(128)S(6)} %copy.11.e_ref), custom_call_target="tpu_custom_call" | custom-call | tf_op jit(solution)/shard_map/filter/pallas_call | solution.py:244
  114.6 0.7 copy.8
  115.3 0.6 copy.9

commit v6 on v5

--- a/solution.py
+++ b/solution.py
@@ -123,7 +123,7 @@
     y0_copy.start()
 
     padding = pl.ds(2 * piece, acc.shape[1] - 2 * piece)
-    tile[:, padding] = jnp.zeros_like(tile[:, padding])
+    tile[:, padding] = jnp.zeros((tile.shape[0], padding.size), jnp.bfloat16)
     barrier = pltpu.get_barrier_semaphore()
     for d in range(1, 8):
         other = lax.rem(me + d, 8)
@@ -171,9 +171,9 @@
                     return sum(parts[1:], parts[0])
 
                 if step == 0 and index == 0:
-                    acc[...] = total(slice(None))
+                    acc[...] = total(pl.ds(0, acc.shape[1]))
                 else:
-                    acc[...] += total(slice(None))
+                    acc[...] += total(pl.ds(0, acc.shape[1]))
         for o in range(CHUNKS):
             partial_copy(par, o).start()
         wait_sends(par)
@@ -247,7 +247,7 @@
             in_specs=[pl.BlockSpec(memory_space=pl.ANY)] * 2 + [pl.BlockSpec(memory_space=pltpu.SMEM)] * 2,
             out_specs=(pl.BlockSpec(memory_space=pltpu.VMEM),) * 2,
             scratch_shapes=[
-                pltpu.VMEM((rows, padded), jnp.bfloat16),
+                pltpu.VMEM((rows, padded + 128), jnp.bfloat16),
                 pltpu.VMEM((2, 5, width, piece), jnp.bfloat16),
                 pltpu.VMEM((2, width, piece), jnp.float32),
                 pltpu.VMEM((width, padded), jnp.float32),

time: 116 us -> 116 us (level)
  no operation moved by 1% of the time
where the time goes in v6:
time: 116 us
  Pallas kernels  112 us (97%)
  between operations  1.93 us (2%)
  local copies, waits for them, and re-layouts  1.35 us (1%)
    pallas_call x1, Pallas kernels, local_filter(): pl.pallas_call(functools.partial(filter_kernel, piece, width), out_shape=...  112 us

profile of v6, /device:TPU:0, one launch (start us, length us, event | category | flops | bytes accessed | tf_op | source)
XLA Modules:
  0.0 115.6 jit_solution(12683628995893721030)
XLA Ops:
  1.9 112.3 %filter.1 = (f32[64,1408]{1,0:T(8,128)S(1)}, f32[64,64]{1,0:T(8,128)S(1)}) custom-call(bf16[5632,2816]{1,0:T(8,128)(2,1)} %a_ref.1, f32[64,1408]{1,0:T(8,128)} %bitcast.3, f32[]{:T(128)S(6)} %copy.10.c_ref, f32[]{:T(128)S(6)} %copy.11.e_ref), custom_call_target="tpu_custom_call" | custom-call | tf_op jit(solution)/shard_map/filter/pallas_call | solution.py:244
  114.2 0.7 copy.8
  115.0 0.6 copy.9

commit v7 on v4

--- a/solution.py
+++ b/solution.py
@@ -15,7 +15,7 @@
 EARLY, LATE = 0, 1
 BLOCKS = (
     (((EARLY, 0, 0),), ((EARLY, 1, 2),), ((LATE, 0, 0), (EARLY, 3, 3)), ((LATE, 1, 1), (EARLY, 4, 5)), ((LATE, 2, 3),), ((LATE, 4, 5),)),
-    (((EARLY, 0, 1),), ((EARLY, 2, 3), (LATE, 0, 0)), ((LATE, 1, 1), (EARLY, 4, 5), (LATE, 2, 2)), ((LATE, 3, 5),)),
+    (((EARLY, 0, 1),), ((EARLY, 2, 3), (LATE, 0, 0)), ((LATE, 1, 1), (EARLY, 4, 5), (LATE, 2, 2)), ((LATE, 3, 4),), ((LATE, 5, 5),)),
 )
 
 
@@ -120,6 +120,8 @@
     y0_copy = pltpu.make_async_copy(y0_ref, state.at[0], y_sem)
     y0_copy.start()
 
+    padding = pl.ds(2 * piece, acc.shape[1] - 2 * piece)
+    tile[:, padding] = jnp.zeros((tile.shape[0], padding.size), jnp.bfloat16)
     barrier = pltpu.get_barrier_semaphore()
     for d in range(1, 8):
         other = lax.rem(me + d, 8)
@@ -159,9 +161,9 @@
                     return sum(parts[1:], parts[0])
 
                 if step == 0 and index == 0:
-                    acc[...] = total(slice(None))
+                    acc[...] = total(pl.ds(0, acc.shape[1]))
                 else:
-                    acc[...] += total(slice(None))
+                    acc[...] += total(pl.ds(0, acc.shape[1]))
         for o in range(CHUNKS):
             partial_copy(par, o).start()
         wait_sends(par)
@@ -228,16 +230,17 @@
     def local_filter(mat_tile, y_start, center, half_width):
         piece, width = y_start.shape
         rows, cols = mat_tile.shape
+        padded = -(-cols // 512) * 512
         y_t, gram = pl.pallas_call(
             functools.partial(filter_kernel, piece, width),
             out_shape=(pltpu.VMEM((width, piece), jnp.float32), pltpu.VMEM((width, width), jnp.float32)),
             in_specs=[pl.BlockSpec(memory_space=pl.ANY)] * 2 + [pl.BlockSpec(memory_space=pltpu.SMEM)] * 2,
             out_specs=(pl.BlockSpec(memory_space=pltpu.VMEM),) * 2,
             scratch_shapes=[
-                pltpu.VMEM((rows, cols), jnp.bfloat16),
+                pltpu.VMEM((rows, padded + 128), jnp.bfloat16),
                 pltpu.VMEM((2, 5, width, piece), jnp.bfloat16),
                 pltpu.VMEM((2, width, piece), jnp.float32),
-                pltpu.VMEM((width, cols), jnp.float32),
+                pltpu.VMEM((width, padded), jnp.float32),
                 pltpu.VMEM((2, width, piece), jnp.float32),
                 pltpu.VMEM((8, width // 2, 2 * width), jnp.float32),
                 pltpu.VMEM((width, piece), jnp.bfloat16),

time: 109 us -> 113 us (1.037)
  Pallas kernels: 105 us -> 110 us
    pallas_call x1, Pallas kernels: 105 us -> 110 us  [local_filter(): pl.pallas_call(functools.partial(filter_kernel, piece, width), out_shape=...]
where the time goes in v7:
time: 113 us
  Pallas kernels  110 us (97%)
  between operations  1.93 us (2%)
  local copies, waits for them, and re-layouts  1.35 us (1%)
    pallas_call x1, Pallas kernels, local_filter(): pl.pallas_call(functools.partial(filter_kernel, piece, width), out_shape=...  110 us

profile of v7, /device:TPU:0, one launch (start us, length us, event | category | flops | bytes accessed | tf_op | source)
XLA Modules:
  0.0 112.8 jit_solution(4460557791555872039)
XLA Ops:
  1.9 109.5 %filter.1 = (f32[64,1408]{1,0:T(8,128)S(1)}, f32[64,64]{1,0:T(8,128)S(1)}) custom-call(bf16[5632,2816]{1,0:T(8,128)(2,1)} %a_ref.1, f32[64,1408]{1,0:T(8,128)} %bitcast.3, f32[]{:T(128)S(6)} %copy.10.c_ref, f32[]{:T(128)S(6)} %copy.11.e_ref), custom_call_target="tpu_custom_call" | custom-call | tf_op jit(solution)/shard_map/filter/pallas_call | solution.py:234
  111.5 0.7 copy.8
  112.2 0.6 copy.9

commit v8 on v4

--- a/solution.py
+++ b/solution.py
@@ -14,7 +14,7 @@
 MESH = pl.DeviceIdType.MESH
 EARLY, LATE = 0, 1
 BLOCKS = (
-    (((EARLY, 0, 0),), ((EARLY, 1, 2),), ((LATE, 0, 0), (EARLY, 3, 3)), ((LATE, 1, 1), (EARLY, 4, 5)), ((LATE, 2, 3),), ((LATE, 4, 5),)),
+    (((EARLY, 0, 0),), ((EARLY, 1, 2),), ((LATE, 0, 0), (EARLY, 3, 3)), ((LATE, 1, 2),), ((EARLY, 4, 5), (LATE, 3, 3)), ((LATE, 4, 5),)),
     (((EARLY, 0, 1),), ((EARLY, 2, 3), (LATE, 0, 0)), ((LATE, 1, 1), (EARLY, 4, 5), (LATE, 2, 2)), ((LATE, 3, 5),)),
 )
 
@@ -40,13 +40,13 @@
     def slot_of(step, kind):
         return pair_base[step] + (core if kind == LATE else sibling)
 
-    def tile_load(step, kind, c, half):
+    def tile_load(step, kind, half):
         col = core if half else sibling
-        rows = pl.ds(pl.multiple_of(slot_of(step, kind) * piece + OFFSETS[c], 128), WIDTHS[c])
+        rows = pl.ds(pl.multiple_of(slot_of(step, kind) * piece, 128), piece)
         return pltpu.make_async_copy(
             a_ref.at[rows, pl.ds(pl.multiple_of(col * piece, 128), piece)],
             tile.at[rows, pl.ds(half * piece, piece)],
-            tile_sem.at[step, kind, c, half],
+            tile_sem.at[step, kind, half],
         )
 
     def slot_view(par, slot, c):
@@ -127,9 +127,8 @@
 
     for step in range(2):
         for kind in (EARLY, LATE):
-            for c in range(CHUNKS):
-                for half in range(2):
-                    tile_load(step, kind, c, half).start()
+            for half in range(2):
+                tile_load(step, kind, half).start()
 
     state[1] = jnp.zeros_like(state[1])
     y0_copy.wait()
@@ -150,9 +149,9 @@
                 for kind, low, high in block:
                     for c in range(low, high + 1):
                         arrive(par, step, kind, c)
-                        if first:
+                        if first and c == 0:
                             for half in range(2):
-                                tile_load(step, kind, c, half).wait()
+                                tile_load(step, kind, half).wait()
 
                 def total(cols):
                     parts = [product(par, slot_of(step, kind), OFFSETS[low], OFFSETS[high] + WIDTHS[high] - OFFSETS[low], cols) for kind, low, high in block]
@@ -241,7 +240,7 @@
                 pltpu.VMEM((2, width, piece), jnp.float32),
                 pltpu.VMEM((8, width // 2, 2 * width), jnp.float32),
                 pltpu.VMEM((width, piece), jnp.bfloat16),
-                pltpu.SemaphoreType.DMA((2, 2, CHUNKS, 2)),
+                pltpu.SemaphoreType.DMA((2, 2, 2)),
                 pltpu.SemaphoreType.DMA((2, 4, CHUNKS)),
                 pltpu.SemaphoreType.DMA((3, CHUNKS)),
                 pltpu.SemaphoreType.DMA((2, CHUNKS)),

time: 109 us -> 110 us (level)
    pallas_call x1, Pallas kernels: 105 us -> 106 us  [local_filter(): pl.pallas_call(functools.partial(filter_kernel, piece, width), out_shape=...]
where the time goes in v8:
time: 110 us
  Pallas kernels  106 us (96%)
  between operations  1.93 us (2%)
  local copies, waits for them, and re-layouts  1.35 us (1%)
    pallas_call x1, Pallas kernels, local_filter(): pl.pallas_call(functools.partial(filter_kernel, piece, width), out_shape=...  106 us

profile of v8, /device:TPU:0, one launch (start us, length us, event | category | flops | bytes accessed | tf_op | source)
XLA Modules:
  0.0 109.6 jit_solution(5551729760570733832)
XLA Ops:
  1.9 106.3 %filter.1 = (f32[64,1408]{1,0:T(8,128)S(1)}, f32[64,64]{1,0:T(8,128)S(1)}) custom-call(bf16[5632,2816]{1,0:T(8,128)(2,1)} %a_ref.1, f32[64,1408]{1,0:T(8,128)} %bitcast.3, f32[]{:T(128)S(6)} %copy.10.c_ref, f32[]{:T(128)S(6)} %copy.11.e_ref), custom_call_target="tpu_custom_call" | custom-call | tf_op jit(solution)/shard_map/filter/pallas_call | solution.py:230
  108.3 0.7 copy.8
  109.0 0.6 copy.9

commit v9 on v4

--- a/solution.py
+++ b/solution.py
@@ -96,6 +96,14 @@
 
     def arrive(par, step, kind, c):
         if step == 1:
+            if kind == EARLY and c % 2 == 0:
+
+                @pl.when(far)
+                def _():
+                    wait_slot(par, slot_of(1, kind), c)
+
+                return
+
             wait_slot(par, slot_of(1, kind), c)
             if (c + kind) % 2 == 0:
 
@@ -147,6 +155,13 @@
     def apply_matrix(par, first, combine):
         for step in range(2):
             for index, block in enumerate(BLOCKS[step]):
+                if step == 0 and index >= 3:
+
+                    @pl.when(near)
+                    def _():
+                        wait_slot(par, slot_of(1, EARLY), 2 * index - 6)
+                        fwd_copy(par, 1, EARLY, 2 * index - 6).start()
+
                 for kind, low, high in block:
                     for c in range(low, high + 1):
                         arrive(par, step, kind, c)

time: 109 us -> 112 us (1.028)
  Pallas kernels: 105 us -> 109 us
    pallas_call x1, Pallas kernels: 105 us -> 109 us  [local_filter(): pl.pallas_call(functools.partial(filter_kernel, piece, width), out_shape=...]
where the time goes in v9:
time: 112 us
  Pallas kernels  109 us (97%)
  between operations  1.93 us (2%)
  local copies, waits for them, and re-layouts  1.35 us (1%)
    pallas_call x1, Pallas kernels, local_filter(): pl.pallas_call(functools.partial(filter_kernel, piece, width), out_shape=...  109 us

profile of v9, /device:TPU:0, one launch (start us, length us, event | category | flops | bytes accessed | tf_op | source)
XLA Modules:
  0.0 111.9 jit_solution(8938006562994375963)
XLA Ops:
  1.9 108.7 %filter.1 = (f32[64,1408]{1,0:T(8,128)S(1)}, f32[64,64]{1,0:T(8,128)S(1)}) custom-call(bf16[5632,2816]{1,0:T(8,128)(2,1)} %a_ref.1, f32[64,1408]{1,0:T(8,128)} %bitcast.3, f32[]{:T(128)S(6)} %copy.10.c_ref, f32[]{:T(128)S(6)} %copy.11.e_ref), custom_call_target="tpu_custom_call" | custom-call | tf_op jit(solution)/shard_map/filter/pallas_call | solution.py:246
  110.6 0.7 copy.8
  111.3 0.6 copy.9

commit v10 on v4

--- a/solution.py
+++ b/solution.py
@@ -17,6 +17,8 @@
     (((EARLY, 0, 0),), ((EARLY, 1, 2),), ((LATE, 0, 0), (EARLY, 3, 3)), ((LATE, 1, 1), (EARLY, 4, 5)), ((LATE, 2, 3),), ((LATE, 4, 5),)),
     (((EARLY, 0, 1),), ((EARLY, 2, 3), (LATE, 0, 0)), ((LATE, 1, 1), (EARLY, 4, 5), (LATE, 2, 2)), ((LATE, 3, 5),)),
 )
+HELD_BACK = ((EARLY, 1), (EARLY, 3), (LATE, 0))
+PASSED_AT_ONCE = ((EARLY, 5), (LATE, 2), (LATE, 4))
 
 
 def filter_kernel(piece, width, a_ref, y0_ref, c_ref, e_ref, y_out, g_out, tile, src, state, acc, prec, gall, image, tile_sem, recv_sem, send_sem, fwd_sem, psend_sem, prec_sem, gsend_sem, grecv_sem, y_sem):
@@ -108,13 +110,13 @@
         if kind == EARLY:
             wait_slot(par, slot_of(0, kind), c)
 
-        if kind == LATE or (c + kind) % 2 == 1:
+        if kind == LATE or (kind, c) in PASSED_AT_ONCE:
 
             @pl.when(far)
             def _():
                 if kind == LATE:
                     wait_slot(par, slot_of(0, kind), c)
-                if (c + kind) % 2 == 1:
+                if (kind, c) in PASSED_AT_ONCE:
                     fwd_copy(par, 0, kind, c).start()
 
     y0_copy = pltpu.make_async_copy(y0_ref, state.at[0], y_sem)
@@ -147,6 +149,13 @@
     def apply_matrix(par, first, combine):
         for step in range(2):
             for index, block in enumerate(BLOCKS[step]):
+                if step == 0 and index == 3:
+
+                    @pl.when(far)
+                    def _():
+                        for kind, c in HELD_BACK:
+                            fwd_copy(par, 0, kind, c).start()
+
                 for kind, low, high in block:
                     for c in range(low, high + 1):
                         arrive(par, step, kind, c)

time: 109 us -> 111 us (1.018)
  Pallas kernels: 105 us -> 107 us
    pallas_call x1, Pallas kernels: 105 us -> 107 us  [local_filter(): pl.pallas_call(functools.partial(filter_kernel, piece, width), out_shape=...]
where the time goes in v10:
time: 111 us
  Pallas kernels  107 us (96%)
  between operations  1.93 us (2%)
  local copies, waits for them, and re-layouts  1.35 us (1%)
    pallas_call x1, Pallas kernels, local_filter(): pl.pallas_call(functools.partial(filter_kernel, piece, width), out_shape=...  107 us

profile of v10, /device:TPU:0, one launch (start us, length us, event | category | flops | bytes accessed | tf_op | source)
XLA Modules:
  0.0 110.7 jit_solution(6684561117671905082)
XLA Ops:
  1.9 107.4 %filter.1 = (f32[64,1408]{1,0:T(8,128)S(1)}, f32[64,64]{1,0:T(8,128)S(1)}) custom-call(bf16[5632,2816]{1,0:T(8,128)(2,1)} %a_ref.1, f32[64,1408]{1,0:T(8,128)} %bitcast.3, f32[]{:T(128)S(6)} %copy.10.c_ref, f32[]{:T(128)S(6)} %copy.11.e_ref), custom_call_target="tpu_custom_call" | custom-call | tf_op jit(solution)/shard_map/filter/pallas_call | solution.py:240
  109.4 0.7 copy.8
  110.1 0.6 copy.9

commit v11 on v4

--- a/solution.py
+++ b/solution.py
@@ -72,12 +72,15 @@
         return remote(acc.at[:, cols], prec.at[par, :, cols], psend_sem.at[o], prec_sem.at[par, o], (chip, sibling))
 
     def send_own(par, c):
-        own_copy(par, c, 0).start()
         own_copy(par, c, 1).start()
 
         @pl.when(far)
         def _():
             own_copy(par, c, 2).start()
+
+    def send_own_x(par):
+        for c in range(CHUNKS):
+            own_copy(par, c, 0).start()
 
     def wait_sends(par):
         for c in range(CHUNKS):
@@ -137,6 +140,7 @@
     pl.semaphore_wait(barrier, 7)
     for c in range(CHUNKS):
         send_own(0, c)
+    send_own_x(0)
     center = c_ref[()]
     half_width = e_ref[()]
 
@@ -144,7 +148,7 @@
         rows = pl.ds(pl.multiple_of(slot * piece + off, 128), size)
         return jnp.dot(src[par, slot, :, pl.ds(off, size)], tile[rows, cols], preferred_element_type=jnp.float32)
 
-    def apply_matrix(par, first, combine):
+    def apply_matrix(par, first, combine, finish):
         for step in range(2):
             for index, block in enumerate(BLOCKS[step]):
                 for kind, low, high in block:
@@ -168,6 +172,7 @@
         for o in range(CHUNKS):
             partial_copy(par, o).wait_recv()
             combine(o, acc[:, pl.ds(piece + OFFSETS[o], WIDTHS[o])] + prec[par, :, pl.ds(OFFSETS[o], WIDTHS[o])])
+        finish()
         for o in range(CHUNKS):
             partial_copy(par, o).wait_send()
 
@@ -185,7 +190,7 @@
             src[other, own_slot, :, cols] = following.astype(jnp.bfloat16)
             send_own(other, o)
 
-        apply_matrix(par, first, combine)
+        apply_matrix(par, first, combine, lambda: send_own_x(other))
 
     advance(0, True)
 
@@ -200,7 +205,7 @@
     def gram_part(o, total):
         image[:, pl.ds(OFFSETS[o], WIDTHS[o])] = total.astype(jnp.bfloat16)
 
-    apply_matrix(0, False, gram_part)
+    apply_matrix(0, False, gram_part, lambda: None)
     gram_part_sum = lax.dot_general(src[0, own_slot], image[...], (((1,), (1,)), ((), ())), preferred_element_type=jnp.float32)
     half = width // 2
     gall[me] = jnp.concatenate([gram_part_sum[:half], gram_part_sum[half:]], axis=1)

time: 109 us -> 109 us (level)
  no operation moved by 1% of the time
where the time goes in v11:
time: 109 us
  Pallas kernels  105 us (96%)
  between operations  1.93 us (2%)
  local copies, waits for them, and re-layouts  1.35 us (1%)
    pallas_call x1, Pallas kernels, local_filter(): pl.pallas_call(functools.partial(filter_kernel, piece, width), out_shape=...  105 us

profile of v11, /device:TPU:0, one launch (start us, length us, event | category | flops | bytes accessed | tf_op | source)
XLA Modules:
  0.0 108.6 jit_solution(8181703284257547570)
XLA Ops:
  1.9 105.3 %filter.1 = (f32[64,1408]{1,0:T(8,128)S(1)}, f32[64,64]{1,0:T(8,128)S(1)}) custom-call(bf16[5632,2816]{1,0:T(8,128)(2,1)} %a_ref.1, f32[64,1408]{1,0:T(8,128)} %bitcast.3, f32[]{:T(128)S(6)} %copy.10.c_ref, f32[]{:T(128)S(6)} %copy.11.e_ref), custom_call_target="tpu_custom_call" | custom-call | tf_op jit(solution)/shard_map/filter/pallas_call | solution.py:236
  107.2 0.7 copy.8
  107.9 0.6 copy.9

commit v12 on v11

--- a/solution.py
+++ b/solution.py
@@ -17,6 +17,7 @@
     (((EARLY, 0, 0),), ((EARLY, 1, 2),), ((LATE, 0, 0), (EARLY, 3, 3)), ((LATE, 1, 1), (EARLY, 4, 5)), ((LATE, 2, 3),), ((LATE, 4, 5),)),
     (((EARLY, 0, 1),), ((EARLY, 2, 3), (LATE, 0, 0)), ((LATE, 1, 1), (EARLY, 4, 5), (LATE, 2, 2)), ((LATE, 3, 5),)),
 )
+NEAR_RELAYS = ((EARLY, 0), (EARLY, 2), (LATE, 1), (LATE, 5))
 
 
 def filter_kernel(piece, width, a_ref, y0_ref, c_ref, e_ref, y_out, g_out, tile, src, state, acc, prec, gall, image, tile_sem, recv_sem, send_sem, fwd_sem, psend_sem, prec_sem, gsend_sem, grecv_sem, y_sem):
@@ -93,14 +94,14 @@
 
             for kind in (EARLY, LATE):
 
-                @pl.when(near if (c + kind) % 2 == 0 else far)
+                @pl.when(near if (kind, c) in NEAR_RELAYS else far)
                 def _():
                     fwd_copy(par, 0, kind, c).wait_send()
 
     def arrive(par, step, kind, c):
         if step == 1:
             wait_slot(par, slot_of(1, kind), c)
-            if (c + kind) % 2 == 0:
+            if (kind, c) in NEAR_RELAYS:
 
                 @pl.when(near)
                 def _():
@@ -111,13 +112,13 @@
         if kind == EARLY:
             wait_slot(par, slot_of(0, kind), c)
 
-        if kind == LATE or (c + kind) % 2 == 1:
+        if kind == LATE or (kind, c) not in NEAR_RELAYS:
 
             @pl.when(far)
             def _():
                 if kind == LATE:
                     wait_slot(par, slot_of(0, kind), c)
-                if (c + kind) % 2 == 1:
+                if (kind, c) not in NEAR_RELAYS:
                     fwd_copy(par, 0, kind, c).start()
 
     y0_copy = pltpu.make_async_copy(y0_ref, state.at[0], y_sem)

time: 109 us -> 108 us (level)
    pallas_call x1, Pallas kernels: 105 us -> 104 us  [local_filter(): pl.pallas_call(functools.partial(filter_kernel, piece, width), out_shape=...]
where the time goes in v12:
time: 108 us; the launch traced here: 107 us
  Pallas kernels  104 us (96%)
  between operations  1.93 us (2%)
  local copies, waits for them, and re-layouts  1.35 us (1%)
    pallas_call x1, Pallas kernels, local_filter(): pl.pallas_call(functools.partial(filter_kernel, piece, width), out_shape=...  104 us

profile of v12, /device:TPU:0, one launch (start us, length us, event | category | flops | bytes accessed | tf_op | source)
XLA Modules:
  0.0 107.4 jit_solution(10018321019065012109)
XLA Ops:
  1.9 104.1 %filter.1 = (f32[64,1408]{1,0:T(8,128)S(1)}, f32[64,64]{1,0:T(8,128)S(1)}) custom-call(bf16[5632,2816]{1,0:T(8,128)(2,1)} %a_ref.1, f32[64,1408]{1,0:T(8,128)} %bitcast.3, f32[]{:T(128)S(6)} %copy.10.c_ref, f32[]{:T(128)S(6)} %copy.11.e_ref), custom_call_target="tpu_custom_call" | custom-call | tf_op jit(solution)/shard_map/filter/pallas_call | solution.py:237
  106.1 0.7 copy.8
  106.8 0.6 copy.9

commit v13 on v12

--- a/solution.py
+++ b/solution.py
@@ -14,7 +14,7 @@
 MESH = pl.DeviceIdType.MESH
 EARLY, LATE = 0, 1
 BLOCKS = (
-    (((EARLY, 0, 0),), ((EARLY, 1, 2),), ((LATE, 0, 0), (EARLY, 3, 3)), ((LATE, 1, 1), (EARLY, 4, 5)), ((LATE, 2, 3),), ((LATE, 4, 5),)),
+    (((EARLY, 0, 0),), ((EARLY, 1, 2),), ((EARLY, 3, 5),), ((LATE, 0, 1),), ((LATE, 2, 3),), ((LATE, 4, 5),)),
     (((EARLY, 0, 1),), ((EARLY, 2, 3), (LATE, 0, 0)), ((LATE, 1, 1), (EARLY, 4, 5), (LATE, 2, 2)), ((LATE, 3, 5),)),
 )
 NEAR_RELAYS = ((EARLY, 0), (EARLY, 2), (LATE, 1), (LATE, 5))

time: 108 us -> 112 us (1.037)
  Pallas kernels: 104 us -> 108 us
    pallas_call x1, Pallas kernels: 104 us -> 108 us  [local_filter(): pl.pallas_call(functools.partial(filter_kernel, piece, width), out_shape=...]
where the time goes in v13:
time: 112 us
  Pallas kernels  108 us (96%)
  between operations  1.93 us (2%)
  local copies, waits for them, and re-layouts  1.35 us (1%)
    pallas_call x1, Pallas kernels, local_filter(): pl.pallas_call(functools.partial(filter_kernel, piece, width), out_shape=...  108 us

profile of v13, /device:TPU:0, one launch (start us, length us, event | category | flops | bytes accessed | tf_op | source)
XLA Modules:
  0.0 111.6 jit_solution(2592289358981514001)
XLA Ops:
  1.9 108.4 %filter.1 = (f32[64,1408]{1,0:T(8,128)S(1)}, f32[64,64]{1,0:T(8,128)S(1)}) custom-call(bf16[5632,2816]{1,0:T(8,128)(2,1)} %a_ref.1, f32[64,1408]{1,0:T(8,128)} %bitcast.3, f32[]{:T(128)S(6)} %copy.10.c_ref, f32[]{:T(128)S(6)} %copy.11.e_ref), custom_call_target="tpu_custom_call" | custom-call | tf_op jit(solution)/shard_map/filter/pallas_call | solution.py:237
  110.3 0.7 copy.8
  111.0 0.6 copy.9

commit v14 on v12

--- a/solution.py
+++ b/solution.py
@@ -47,8 +47,12 @@
         return pltpu.make_async_copy(
             a_ref.at[rows, pl.ds(pl.multiple_of(col * piece, 128), piece)],
             tile.at[rows, pl.ds(half * piece, piece)],
-            tile_sem.at[step, kind, c, half],
+            tile_sem.at[step, kind, c],
         )
+
+    def wait_tile(step, kind, c):
+        rows = pl.ds(pl.multiple_of(slot_of(step, kind) * piece + OFFSETS[c], 128), WIDTHS[c])
+        pltpu.make_async_copy(a_ref.at[rows], tile.at[rows], tile_sem.at[step, kind, c]).wait()
 
     def slot_view(par, slot, c):
         return src.at[par, slot, :, pl.ds(OFFSETS[c], WIDTHS[c])]
@@ -156,8 +160,7 @@
                     for c in range(low, high + 1):
                         arrive(par, step, kind, c)
                         if first:
-                            for half in range(2):
-                                tile_load(step, kind, c, half).wait()
+                            wait_tile(step, kind, c)
 
                 def total(cols):
                     parts = [product(par, slot_of(step, kind), OFFSETS[low], OFFSETS[high] + WIDTHS[high] - OFFSETS[low], cols) for kind, low, high in block]
@@ -247,7 +250,7 @@
                 pltpu.VMEM((2, width, piece), jnp.float32),
                 pltpu.VMEM((8, width // 2, 2 * width), jnp.float32),
                 pltpu.VMEM((width, piece), jnp.bfloat16),
-                pltpu.SemaphoreType.DMA((2, 2, CHUNKS, 2)),
+                pltpu.SemaphoreType.DMA((2, 2, CHUNKS)),
                 pltpu.SemaphoreType.DMA((2, 4, CHUNKS)),
                 pltpu.SemaphoreType.DMA((3, CHUNKS)),
                 pltpu.SemaphoreType.DMA((2, CHUNKS)),

time: 108 us -> 107 us (level)
  no operation moved by 1% of the time
where the time goes in v14:
time: 107 us
  Pallas kernels  104 us (97%)
  between operations  1.93 us (2%)
  local copies, waits for them, and re-layouts  1.35 us (1%)
    pallas_call x1, Pallas kernels, local_filter(): pl.pallas_call(functools.partial(filter_kernel, piece, width), out_shape=...  104 us

profile of v14, /device:TPU:0, one launch (start us, length us, event | category | flops | bytes accessed | tf_op | source)
XLA Modules:
  0.0 107.2 jit_solution(5821347451797113157)
XLA Ops:
  1.9 103.9 %filter.1 = (f32[64,1408]{1,0:T(8,128)S(1)}, f32[64,64]{1,0:T(8,128)S(1)}) custom-call(bf16[5632,2816]{1,0:T(8,128)(2,1)} %a_ref.1, f32[64,1408]{1,0:T(8,128)} %bitcast.3, f32[]{:T(128)S(6)} %copy.10.c_ref, f32[]{:T(128)S(6)} %copy.11.e_ref), custom_call_target="tpu_custom_call" | custom-call | tf_op jit(solution)/shard_map/filter/pallas_call | solution.py:240
  105.8 0.7 copy.8
  106.6 0.6 copy.9
